TPU v7x, 128 devices: a whole 4x4x4 slice. The times are simulated.
128 devices in a mesh: row: 16 (over z, y), col: 8 (over x, core).
Axes of the slice: x: 4, y: 4, z: 4, core: 2. Of those that a mesh axis runs over, the one named last changes fastest.
Arguments:
- inv_interior: bfloat16 [512, 1024, 1024], P(('row', 'col')), may hold values from -1 to 3
- coupling: bfloat16 [512, 1024, 512], P(('row', 'col')), may hold values from -0.375 to 0.375
- boundary_stiff: bfloat16 [512, 512, 512], P(('row', 'col')), may hold values from -6 to 6
- mass_interior: float32 [512, 1024], P(('row', 'col')), may hold values from 0.5 to 2
- mass_boundary: float32 [512, 512], P(('row', 'col')), may hold values from 0.5 to 2
- block_map: int32 [512, 4], P(('row', 'col')), may hold values from 0 to 127, as said below
- modes: bfloat16 [16384, 1024], P('col', 'row'), may hold values from -0.046875 to 0.046875
Outputs:
- iface_stiff: bfloat16 [16384, 16384], P('row', 'col')
- iface_mass: bfloat16 [16384, 16384], P('row', 'col')
- reduced_stiff: float32 [1024, 1024], P(('row', 'col'))
- reduced_mass: float32 [1024, 1024], P(('row', 'col'))
- mass_diagonal: float32 [16384], P(('row', 'col'))
Inputs may be any that keep to these rules, and one draw needn't show every extreme that they name: Interface block p belongs to tile row p // 8 and tile column p // 16; the pair (block_map[s, a], block_map[s, b]) belongs to the tile of its row's tile row and its column's tile column. Over the 4 substructures of one device (aligned blocks of rows), no two triples (s, a, b) fall into the same tile, and in every draw some tile receives a pair from every device.
All inputs are finite; a program needn't handle non-finite values.
Results may differ from a plain program's by a relative error of at most 0.0058.
Values may be sent and summed in bfloat16 or wider, within the bound.
A program may use at most 192 MiB of HBM per device.

v0:
```python
import jax
import jax.numpy as jnp
from jax import lax
from jax.sharding import Mesh
from jax.sharding import PartitionSpec as P

BLK = 128
ROW = ("row_0", "row_1")
COL = ("col_0", "col_1")
ROW_COL = ("row_0", "row_1", "col_0", "col_1")


def cut_along(x, dim, devices):
    before, after = (x.shape[:dim], x.shape[dim + 1 :])
    return jnp.moveaxis(x.reshape(*before, devices, -1, *after), dim, 0)


def summed_on_arrival(x, axis, dim):
    devices = lax.axis_size(axis)
    pieces = lax.all_to_all(cut_along(x, dim, devices), axis, 0, 0, tiled=True)
    return jnp.sum(pieces, axis=0)


def from_root(x, axes, root):
    x = jnp.where(lax.axis_index(axes) == root, x, jnp.zeros_like(x))
    for axis in axes:
        x = lax.psum(x, axis)
    return x


def summed_on_arrival_2(x, axis, dim):
    pieces = cut_along(x, dim, lax.axis_size(axis))
    arrived = lax.all_to_all(pieces, axis, split_axis=0, concat_axis=0, tiled=True)
    return arrived.astype(jnp.float32).sum(axis=0)


def summed_rows(x, axes, dim):
    far, near = axes
    pieces = cut_along(x, dim, lax.axis_size(far))
    nearer = summed_on_arrival_2(pieces, near, dim + 1)
    arrived = lax.all_to_all(
        nearer.astype(jnp.bfloat16), far, split_axis=0, concat_axis=0, tiled=True
    )
    return arrived.astype(jnp.float32).sum(axis=0)


def condense(pieces):
    inverse, couple, stiffness, interior_mass, boundary_mass = pieces
    static_modes = (-jnp.dot(inverse, couple, preferred_element_type=jnp.float32)).astype(
        jnp.bfloat16
    )
    stiff_cond = stiffness.astype(jnp.float32) + jnp.dot(
        couple.T, static_modes, preferred_element_type=jnp.float32
    )
    weighted = (static_modes.astype(jnp.float32) * interior_mass[:, None]).astype(jnp.bfloat16)
    mass_cond = jnp.dot(static_modes.T, weighted, preferred_element_type=jnp.float32) + jnp.diag(
        boundary_mass
    )
    return jnp.stack([stiff_cond, mass_cond])


def body(inv_interior, coupling, boundary_stiff, mass_interior, mass_boundary, block_map, modes):
    row_count = lax.axis_size(ROW)
    col_count = lax.axis_size(COL)
    device_count = row_count * col_count
    local_subs, interior_width, boundary_width = coupling.shape
    per_sub = boundary_width // BLK
    tile_cols = modes.shape[0]
    tile_rows = tile_cols * col_count // row_count
    mode_count = modes.shape[1] * row_count
    row_blocks = tile_rows // BLK
    col_blocks = tile_cols // BLK
    row_index = lax.axis_index(ROW)
    col_index = lax.axis_index(COL)
    ratio_rows = row_count // col_count
    share_rows = tile_rows // col_count
    condensed = lax.map(
        condense, (inv_interior, coupling, boundary_stiff, mass_interior, mass_boundary)
    )
    blocks = condensed.reshape(local_subs, 2, per_sub, BLK, per_sub, BLK).transpose(
        0, 2, 4, 1, 3, 5
    )
    blocks = blocks.reshape(local_subs * per_sub * per_sub, 2, BLK, BLK)
    block_rows = jnp.broadcast_to(block_map[:, :, None], (local_subs, per_sub, per_sub)).reshape(-1)
    block_cols = jnp.broadcast_to(block_map[:, None, :], (local_subs, per_sub, per_sub)).reshape(-1)
    owner_index = block_rows // row_blocks * col_count + block_cols // col_blocks
    slot_index = block_rows % row_blocks * col_blocks + block_cols % col_blocks
    matches = owner_index[None, :] == jnp.arange(device_count, dtype=jnp.int32)[:, None]
    filled = jnp.any(matches, axis=1)
    chosen = jnp.argmax(matches, axis=1)
    outgoing = jnp.take(blocks, chosen, axis=0) * filled[:, None, None, None].astype(jnp.float32)
    targets = jnp.where(filled, jnp.take(slot_index, chosen), -1)
    arrived, arrived_slots = (
        lax.all_to_all(
            outgoing.astype(jnp.bfloat16), ROW_COL, split_axis=0, concat_axis=0, tiled=True
        ).astype(outgoing.dtype),
        lax.all_to_all(targets, ROW_COL, split_axis=0, concat_axis=0, tiled=True),
    )
    summed_blocks = jax.ops.segment_sum(
        arrived, jnp.maximum(arrived_slots, 0), num_segments=row_blocks * col_blocks
    )
    full_pair = summed_blocks.reshape(row_blocks, col_blocks, 2, BLK, BLK).transpose(2, 0, 3, 1, 4)
    full_pair = full_pair.reshape(2, tile_rows, tile_cols)
    holder = col_index == row_index // ratio_rows
    offset = row_index % ratio_rows * tile_rows
    column_ids = jnp.arange(tile_cols, dtype=jnp.int32)[None, :]
    row_ids = jnp.arange(tile_rows, dtype=jnp.int32)[:, None]
    on_diagonal = jnp.logical_and(column_ids == row_ids + offset, holder)
    mass_tile = full_pair[1]
    diag_local = jnp.sum(jnp.where(on_diagonal, mass_tile, jnp.float32(0.0)), axis=1)
    mass_share = summed_on_arrival(diag_local, COL, 0)
    stiff_tile = full_pair[0].astype(jnp.bfloat16)
    mass_off = jnp.where(on_diagonal, jnp.float32(0.0), mass_tile).astype(jnp.bfloat16)
    col_modes = lax.all_gather(modes, ROW, axis=1, tiled=True)
    mode_slab = lax.dynamic_slice_in_dim(
        col_modes, row_index % ratio_rows * tile_rows, tile_rows, 0
    )
    row_modes = from_root(mode_slab, COL, row_index // ratio_rows)
    right_side = jnp.concatenate(
        [
            jnp.dot(stiff_tile, col_modes, preferred_element_type=jnp.float32),
            jnp.dot(mass_off, col_modes, preferred_element_type=jnp.float32),
        ],
        1,
    )
    left_modes = row_modes.astype(jnp.float32)
    share_start = col_index * share_rows
    share_modes = lax.dynamic_slice_in_dim(left_modes, share_start, share_rows, 0)
    mass_part = lax.dynamic_slice(
        right_side, (share_start, jnp.int32(mode_count)), (share_rows, mode_count)
    )
    right_side = lax.dynamic_update_slice(
        right_side,
        mass_part + mass_share[:, None] * share_modes,
        (share_start, jnp.int32(mode_count)),
    )
    reduced = summed_rows(
        jnp.dot(
            left_modes.T,
            right_side,
            precision=lax.Precision.HIGHEST,
            preferred_element_type=jnp.float32,
        ).astype(jnp.bfloat16),
        (("row_0", "row_1", "col_0"), "col_1"),
        0,
    )
    return (stiff_tile, mass_off, reduced[:, :mode_count], reduced[:, mode_count:], mass_share)


def solution(mesh):
    finer = Mesh(mesh.devices.reshape(4, 4, 4, 2), ("row_0", "row_1", "col_0", "col_1"))
    placed = (
        P(ROW_COL, None, None),
        P(ROW_COL, None, None),
        P(ROW_COL, None, None),
        P(ROW_COL, None),
        P(ROW_COL, None),
        P(ROW_COL, None),
        P(COL, ROW),
    )
    return jax.shard_map(
        body,
        mesh=finer,
        in_specs=placed,
        out_specs=(P(ROW, COL), P(ROW, COL), P(ROW_COL, None), P(ROW_COL, None), P(ROW_COL)),
        check_vma=False,
    )
```

profile of v0, /device:TPU:1, one launch (start us, length us, event | category | flops | bytes accessed | tf_op | source)
XLA Modules:
  0.0 436.3 jit_solution(2629234917405729880)
XLA Ops:
  11.5 11.5 %all-to-all-start = ((s32[128,1,1]{2,1,0:T(1,128)}), s32[128,1,1]{2,1,0:T(1,128)S(1)}, u32[]{:S(2)}, u32[]{:S(2)}) async-start(s32[128,1,1]{2,1,0:T(1,128)} %copy.25), calls=%async_computation | async-start | bytes 131072 | tf_op jit(solution)/shard_map/all_to_all | solution.py:97
  23.0 36.2 %while.10 = (s32[]{:T(128)}, f32[4,2,512,512]{3,2,1,0:T(8,128)}, bf16[4,512,512]{2,1,0:T(8,128)(2,1)}, bf16[4,1024,512]{2,1,0:T(8,128)(2,1)}, bf16[4,1024,1024]{...) while((s32[]{:T(128)}, f32[4,2,512,512]{3,2,1,0:T(8,128)}, ...), condition=%wide.region_3.4_spmd, body=%wide.region_2.3_spmd.sunk | while | flops 2151940096 | bytes 14176361 | solution.py:77
  23.1 3.1 negate_convert_fusion.2
  32.2 3.1 negate_convert_fusion.2
  41.1 3.1 negate_convert_fusion.2
  50.2 3.1 negate_convert_fusion.2
  59.2 9.9 %reshape.163 = f32[4,2,4,128,4,128]{5,4,3,2,1,0:T(4,128)} reshape(f32[4,2,512,512]{3,2,1,0:T(8,128)} %get-tuple-element.44) | data formatting | bytes 16777216 | tf_op jit(solution)/shard_map/reshape | solution.py:80
  69.1 7.8 %copy.26 = f32[4,4,4,2,128,128]{5,4,3,2,1,0:T(8,128)} copy(f32[4,4,4,2,128,128]{5,2,4,1,3,0:T(4,128)} %bitcast.83) | data formatting | bytes 16777216 | tf_op jit(solution)/shard_map/transpose | solution.py:80
  76.9 13.1 %gather_fusion.1 = f32[128,2,128,128]{3,2,1,0:T(8,128)} fusion(f32[64,2,128,128]{3,2,1,0:T(8,128)} %bitcast.82, s32[1024]{0:T(1024)S(1)} %pad_clamp_fusion), kind=kCustom, calls=%fused_computation.1 | custom fusion | bytes 33554944 | tf_op jit(solution)/shard_map/jit(_take)/gather | solution.py:91
  90.0 10.0 %multiply_convert_fusion.6 = bf16[128,2,128,128]{3,2,1,0:T(8,128)(2,1)} fusion(f32[128,2,128,128]{3,2,1,0:T(8,128)} %gather_fusion.1, f32[128]{0:T(128)S(1)} %convert_element_type.47, pred[128]{0:T(512)(128)(4,1)S(1)} %get-tuple-element.60), kind=kLoop, calls=%fused_computation.25 | loop fusion | flops 12582912 | bytes 25166464 | tf_op jit(solution)/shard_map/convert_element_type | solution.py:95
  100.1 10.2 %all-to-all-start.1 = ((bf16[128,2,128,128]{3,2,1,0:T(8,128)(2,1)}), bf16[128,2,128,128]{3,2,1,0:T(8,128)(2,1)}, u32[]{:S(2)}, u32[]{:S(2)}) async-start(bf16[128,2,128,128]{3,2,1,0:T(8,128)(2,1)} %multiply_convert_fusion.6), calls=%async_computation.1 | async-start | bytes 16777216 | tf_op jit(solution)/shard_map/all_to_all | solution.py:94
  111.0 11.5 %all-reduce.3.cloned.1.call-start = ((), (), s32[]{:S(2)}) async-start(), calls=%async_computation.6 | async-start | bytes 4194304 | tf_op jit(solution)/shard_map/psum | solution.py:27
  122.5 114.5 %all-gather.2.cloned.1.call-done = bf16[2048,1024]{0,1:T(8,128)(2,1)} async-done(((bf16[2048,64]{0,1:T(8,128)(2,1)}), bf16[2048,1024]{0,1:T(8,128)(2,1)}) %all-gather.2.cloned.1.call-update) | async-done | bytes 4194320 | tf_op jit(solution)/shard_map/all_gather | solution.py:114
  237.1 3.4 dynamic-slice_select_fusion
  242.9 11.3 %convert_element_type.49 = f32[128,2,128,128]{3,2,1,0:T(8,128)} convert(bf16[128,2,128,128]{3,2,1,0:T(8,128)(2,1)} %all-to-all-done.1) | non-fusion elementwise | flops 4194304 | bytes 25165824 | tf_op jit(solution)/shard_map/convert_element_type | solution.py:96
  254.2 7.9 %broadcast_in_dim.83 = f32[128,2,128,128]{3,2,1,0:T(8,128)} broadcast(f32[]{:T(128)} %constant.140.clone.1), dimensions={} | broadcast | bytes 16777220 | tf_op jit(solution)/shard_map/broadcast_in_dim | solution.py:99
  262.1 37.0 %scatter_fusion = f32[128,2,128,128]{3,2,1,0:T(8,128)} fusion(f32[128,2,128,128]{3,2,1,0:T(8,128)} %broadcast_in_dim.83, s32[128]{0:T(128)S(1)} %maximum_reduce_fusion, f32[128,2,128,128]{3,2,1,0:T(8,128)} %convert_element_type.49), kind=kCustom, calls=%fused_computation.2 | custom fusion | flops 4194304 | bytes 50332160 | tf_op jit(solution)/shard_map/scatter-add | solution.py:99
  299.0 7.0 %fusion.23 = (bf16[1,8,128,16,128]{4,2,0,3,1:T(8,128)(2,1)S(1)}, bf16[1,8,128,16,128]{4,2,0,3,1:T(8,128)(2,1)S(1)}) fusion(f32[2,8,128,16,128]{4,2,0,3,1:T(8,128)} %bitcast.78), kind=kLoop, calls=%fused_computation.66 | loop fusion | bytes 16777216 | tf_op jit(solution)/shard_map/slice | solution.py:109
  306.1 2.7 copy.27
  308.8 4.2 copy.35
  313.0 4.8 %copy.28 = bf16[1,8,128,16,128]{4,3,2,1,0:T(8,128)(2,1)} copy(bf16[1,8,128,16,128]{4,2,0,3,1:T(8,128)(2,1)S(1)} %get-tuple-element.61) | data formatting | bytes 8388608 | tf_op jit(solution)/shard_map/slice | solution.py:109
  317.8 2.5 select_reduce_fusion
  320.3 5.5 %all-to-all-start.2 = ((f32[8,1,128]{2,1,0:T(1,128)}), f32[8,1,128]{2,1,0:T(1,128)S(1)}, u32[]{:S(2)}, u32[]{:S(2)}) async-start(f32[8,1,128]{2,1,0:T(1,128)} %bitcast.14), calls=%async_computation.2 | async-start | bytes 8192 | tf_op jit(solution)/shard_map/all_to_all | solution.py:20
  325.9 6.7 %fusion.17 = bf16[1024,2048]{1,0:T(8,128)(2,1)} fusion(bf16[128,8,16,128]{3,2,1,0:T(8,128)(2,1)} %bitcast.86, s32[1024]{0:T(1024)S(1)} %iota_add_fusion, pred[]{:T(512)S(6)} %eq.67), kind=kLoop, calls=%fused_computation.30 | loop fusion | flops 6291456 | bytes 8392705 | tf_op jit(solution)/shard_map/convert_element_type | solution.py:113
  332.6 7.7 %fusion.26 = f32[1024,1024]{0,1:T(8,128)S(1)} fusion(bf16[1024,2048]{1,0:T(8,128)(2,1)} %fusion.17, bf16[2048,1024]{0,1:T(8,128)(2,1)} %all-gather.2.cloned.1.call-done), kind=kOutput, calls=%fused_computation.69 | convolution fusion | flops 4294967296 | bytes 12582912 | tf_op jit(solution)/shard_map/dot_general | solution.py:122
  340.4 4.5 %fusion.25 = f32[1024,1024]{0,1:T(8,128)S(1)} fusion(bf16[1024,2048]{1,0:T(8,128)(2,1)S(1)} %bitcast.88, bf16[2048,1024]{0,1:T(8,128)(2,1)S(1)} %copy-done.3), kind=kOutput, calls=%fused_computation.68 | convolution fusion | flops 4294967296 | bytes 12582912 | tf_op jit(solution)/shard_map/dot_general | solution.py:121
  346.9 4.1 pad_maximum_fusion
  351.0 8.5 %all-reduce.5.cloned.1.call-done = bf16[1024,1024]{0,1:T(8,128)(2,1)} async-done(((bf16[1024,1024]{0,1:T(8,128)(2,1)}), bf16[1024,1024]{0,1:T(8,128)(2,1)}) %all-reduce.5.cloned.1.call-update) | async-done | bytes 2097168 | tf_op jit(solution)/shard_map/psum | solution.py:27
  361.7 15.8 %convolution_convert_fusion = bf16[1024,2048]{1,0:T(8,128)(2,1)S(1)} fusion(bf16[1024,1024]{0,1:T(8,128)(2,1)S(1)} %copy-done.4, f32[1024,2048]{0,1:T(8,128)} %add_dynamic-update-slice_fusion), kind=kOutput, calls=%fused_computation.38 | convolution fusion | flops 25771900928 | bytes 14680064 | tf_op jit(solution)/shard_map/dot_general | solution.py:138
  378.1 8.0 %all_to_all.30 = bf16[2,64,8,2048]{3,2,1,0:T(8,128)(2,1)} all-to-all(bf16[2,64,8,2048]{3,2,1,0:T(8,128)(2,1)S(1)} %bitcast.85), channel_id=1, replica_groups=mesh['row_0'=4,'row_1'=4,'col_0'=4,'col_1'=2] {'col_1'}, dimensions={0} | all-to-all | bytes 8388608 | tf_op jit(solution)/shard_map/all_to_all | solution.py:33
  386.1 3.4 reduce_sum.41
  389.5 38.9 %all_to_all.31 = bf16[64,8,2048]{2,1,0:T(8,128)(2,1)S(1)} all-to-all(bf16[64,8,2048]{2,1,0:T(8,128)(2,1)S(1)} %reduce_sum.41), channel_id=1, replica_groups=mesh['row_0'=4,'row_1'=4,'col_0'=4,'col_1'=2] {'row_0','row_1','col_0'}, dimensions={0} | all-to-all | bytes 4194304 | tf_op jit(solution)/shard_map/all_to_all | solution.py:41
  (73 shorter events, 36.8 us)
Async XLA Ops:
  11.5 88.5 %all-to-all-start = ((s32[128,1,1]{2,1,0:T(1,128)}), s32[128,1,1]{2,1,0:T(1,128)S(1)}, u32[]{:S(2)}, u32[]{:S(2)}) async-start(s32[128,1,1]{2,1,0:T(1,128)} %copy.25), calls=%async_computation | async-start | bytes 131072 | tf_op jit(solution)/shard_map/all_to_all | solution.py:97
  100.1 142.8 %all-to-all-start.1 = ((bf16[128,2,128,128]{3,2,1,0:T(8,128)(2,1)}), bf16[128,2,128,128]{3,2,1,0:T(8,128)(2,1)}, u32[]{:S(2)}, u32[]{:S(2)}) async-start(bf16[128,2,128,128]{3,2,1,0:T(8,128)(2,1)} %multiply_convert_fusion.6), calls=%async_computation.1 | async-start | bytes 16777216 | tf_op jit(solution)/shard_map/all_to_all | solution.py:94
  110.2 126.8 %all-gather.2.cloned.1.call-start = ((), (), s32[]{:S(2)}) async-start(), calls=%async_computation.5 | async-start | bytes 4456448 | tf_op jit(solution)/shard_map/all_gather | solution.py:114
  111.0 221.6 %all-reduce.3.cloned.1.call-start = ((), (), s32[]{:S(2)}) async-start(), calls=%async_computation.6 | async-start | bytes 4194304 | tf_op jit(solution)/shard_map/psum | solution.py:27
  299.0 18.8 %slice-start = ((s8[16777216]{0:T(1024)(128)(4,1)}), s8[4194304]{0:T(1024)(128)(4,1)S(1)}, s32[]{:S(2)}) async-start(s8[16777216]{0:T(1024)(128)(4,1)} %bitcast.79), calls=%async_computation.8 | async-start | bytes 8388608
  299.0 18.8 %slice-start.1 = ((s8[16777216]{0:T(1024)(128)(4,1)}), s8[4194304]{0:T(1024)(128)(4,1)S(1)}, s32[]{:S(2)}) async-start(s8[16777216]{0:T(1024)(128)(4,1)} %bitcast.79), calls=%async_computation.9 | async-start | bytes 8388608
  306.1 11.7 %slice-start.2 = ((s8[16777216]{0:T(1024)(128)(4,1)}), s8[4194304]{0:T(1024)(128)(4,1)S(1)}, s32[]{:S(2)}) async-start(s8[16777216]{0:T(1024)(128)(4,1)} %bitcast.79), calls=%async_computation.10 | async-start | bytes 8388608
  308.8 9.0 %slice-start.3 = ((s8[16777216]{0:T(1024)(128)(4,1)}), s8[4194304]{0:T(1024)(128)(4,1)S(1)}, s32[]{:S(2)}) async-start(s8[16777216]{0:T(1024)(128)(4,1)} %bitcast.79), calls=%async_computation.11 | async-start | bytes 8388608
  320.3 30.7 %all-to-all-start.2 = ((f32[8,1,128]{2,1,0:T(1,128)}), f32[8,1,128]{2,1,0:T(1,128)S(1)}, u32[]{:S(2)}, u32[]{:S(2)}) async-start(f32[8,1,128]{2,1,0:T(1,128)} %bitcast.14), calls=%async_computation.2 | async-start | bytes 8192 | tf_op jit(solution)/shard_map/all_to_all | solution.py:20
  325.9 33.7 %all-reduce.5.cloned.1.call-start = ((), (), s32[]{:S(2)}) async-start(), calls=%async_computation.7 | async-start | bytes 4194304 | tf_op jit(solution)/shard_map/psum | solution.py:27
  332.6 7.8 %copy-start.2 = (bf16[128,8,16,128]{3,1,2,0:T(8,128)(2,1)S(1)}, bf16[128,8,16,128]{3,1,2,0:T(8,128)(2,1)}, u32[]{:S(2)}) copy-start(bf16[128,8,16,128]{3,1,2,0:T(8,128)(2,1)} %copy.35) | copy-start | bytes 12582916
  332.6 7.8 %copy-start.3 = (bf16[2048,1024]{0,1:T(8,128)(2,1)S(1)}, bf16[2048,1024]{0,1:T(8,128)(2,1)}, u32[]{:S(2)}) copy-start(bf16[2048,1024]{0,1:T(8,128)(2,1)} %all-gather.2.cloned.1.call-done) | copy-start | bytes 12582916
  340.4 4.6 %copy-start = (f32[1024,1024]{0,1:T(8,128)}, f32[1024,1024]{0,1:T(8,128)S(1)}, u32[]{:S(2)}) copy-start(f32[1024,1024]{0,1:T(8,128)S(1)} %fusion.26) | copy-start | bytes 12582916
  345.0 2.0 copy-start.1
  351.0 10.7 %copy-start.5 = (f32[128]{0:T(128)}, f32[128]{0:T(128)S(1)}, u32[]{:S(2)}) copy-start(f32[128]{0:T(128)S(1)} %reduce_sum.40) | copy-start | bytes 1540
  359.5 2.2 copy-start.4
Sparse Core Ops, SparseCore 0:
  113.2 123.8 all-gather.1
  240.6 58.1 all-reduce.2
  332.7 26.7 all-reduce.4
where the time goes:
time: 444 us; the launch traced here: 436 us
  waiting for transfers between devices  124 us (28%)
  other arithmetic  90.1 us (20%)
  local copies, waits for them, and re-layouts  69.9 us (16%)
  matrix products  52.3 us (12%)
  blocking collectives  46.9 us (11%)
  starting transfers between devices  38.7 us (9%)
  between operations  14.4 us (3%)
    all_gather x1, waiting for transfers between devices, body(): col_modes = lax.all_gather(modes, ROW, axis=1, tiled=True)  115 us
    all_to_all x1, blocking collectives, summed_rows(): lax.all_to_all(nearer.astype(jnp.bfloat16), far, split_axis=0, concat_axi...  38.9 us
    scatter-add x1, other arithmetic, body(): jax.ops.segment_sum(arrived, jnp.maximum(arrived_slots, 0), num_segments=...  37 us
    dot_general x1, matrix products, body(): jnp.dot(left_modes.T, right_side, precision=lax.Precision.HIGHEST, prefer...  15.8 us
    gather x1, local copies, waits for them, and re-layouts, body(): jnp.take(blocks, chosen, axis=0)  13.1 us
    dot_general x4, matrix products, condense(): jnp.dot(inverse, couple, preferred_element_type=jnp.float32)  12.4 us
    slice x2, local copies, waits for them, and re-layouts, body(): mass_tile = full_pair[1]  11.8 us
    all_to_all x1, starting transfers between devices, body(): lax.all_to_all(targets, ROW_COL, split_axis=0, concat_axis=0, tiled=True)  11.5 us
  transfers between devices with their start and end apart: 6, of which 2 were waited for; matrix products, arithmetic and copies ran while one was open for 42% of the time, Pallas kernels for 0%

commit v1 on v0

v1 whole, which is shorter than its diff:
```python
import functools

import jax
import jax.numpy as jnp
from jax import lax
from jax.experimental import pallas as pl
from jax.experimental.pallas import tpu as pltpu
from jax.sharding import PartitionSpec as P

MESH = pl.DeviceIdType.MESH
BLK = 128
F32 = jnp.float32
BF16 = jnp.bfloat16
I32 = jnp.int32
ANY = pl.BlockSpec(memory_space=pl.ANY)
VMEM = pl.BlockSpec(memory_space=pltpu.VMEM)
DMA = pltpu.SemaphoreType.DMA
ROW_OFFS = [(dz, dy) for dz in range(4) for dy in range(4)]
COL_OFFS = [(dx, dk) for dx in range(4) for dk in range(2)]


class Place:
    def __init__(self):
        self.row = lax.axis_index("row")
        self.col = lax.axis_index("col")
        self.z, self.y = lax.div(self.row, 4), lax.rem(self.row, 4)
        self.x, self.k = lax.div(self.col, 2), lax.rem(self.col, 2)

    def row_at(self, dz, dy):
        return lax.rem(self.z + dz, 4) * 4 + lax.rem(self.y + dy, 4)

    def col_at(self, dx, dk):
        return lax.rem(self.x + dx, 4) * 2 + lax.rem(self.k + dk, 2)


def condense_kernel(
    map_ref, inv_ref, couple_ref, stiff_ref, mi_ref, mb_ref, a_ref, b_ref, ma_ref, mb_out_ref
):
    s = pl.program_id(0)
    inverse = inv_ref[0]
    couple = couple_ref[0]
    static = (-jnp.dot(inverse, couple, preferred_element_type=F32)).astype(BF16)
    stiff = stiff_ref[0].astype(F32) + lax.dot_general(
        couple, static, (((0,), (0,)), ((), ())), preferred_element_type=F32
    )
    static_t = static.T
    weighted_t = (static_t.astype(F32) * mi_ref[0]).astype(BF16)
    mass = lax.dot_general(
        static_t, weighted_t, (((1,), (1,)), ((), ())), preferred_element_type=F32
    )
    width = mass.shape[0]
    row_ids = lax.broadcasted_iota(I32, (width, width), 0)
    col_ids = lax.broadcasted_iota(I32, (width, width), 1)
    mass = mass + jnp.where(row_ids == col_ids, mb_ref[0], F32(0.0))
    stiff = stiff.astype(BF16)
    mass = mass.astype(BF16)
    lines = lax.broadcasted_iota(I32, (8, BLK), 0)
    ids = [map_ref[s, a] for a in range(4)]
    table = jnp.zeros((8, BLK), I32)
    for a in range(4):
        table = jnp.where(lines == a, ids[a], table)
    for a in range(4):
        own = jnp.where(lines >= 4, ids[a], table)
        tile_row = ids[a] // 8
        a_ref[tile_row] = stiff[a * BLK : (a + 1) * BLK, :]
        ma_ref[tile_row] = own
        b_ref[tile_row] = mass[:, a * BLK : (a + 1) * BLK]
        mb_out_ref[tile_row] = own


def condense(inv_interior, coupling, boundary_stiff, mass_interior, mass_boundary, block_map):
    subs, inner, edge = coupling.shape
    return pl.pallas_call(
        condense_kernel,
        grid_spec=pltpu.PrefetchScalarGridSpec(
            num_scalar_prefetch=1,
            grid=(subs,),
            in_specs=[
                pl.BlockSpec((1, inner, inner), lambda s, m: (s, 0, 0)),
                pl.BlockSpec((1, inner, edge), lambda s, m: (s, 0, 0)),
                pl.BlockSpec((1, edge, edge), lambda s, m: (s, 0, 0)),
                pl.BlockSpec((1, 1, inner), lambda s, m: (s, 0, 0)),
                pl.BlockSpec((1, 1, edge), lambda s, m: (s, 0, 0)),
            ],
            out_specs=[
                pl.BlockSpec((16, BLK, edge), lambda s, m: (0, 0, 0)),
                pl.BlockSpec((16, edge, BLK), lambda s, m: (0, 0, 0)),
                pl.BlockSpec((16, 8, BLK), lambda s, m: (0, 0, 0)),
                pl.BlockSpec((16, 8, BLK), lambda s, m: (0, 0, 0)),
            ],
        ),
        out_shape=[
            jax.ShapeDtypeStruct((16, BLK, edge), BF16),
            jax.ShapeDtypeStruct((16, edge, BLK), BF16),
            jax.ShapeDtypeStruct((16, 8, BLK), I32),
            jax.ShapeDtypeStruct((16, 8, BLK), I32),
        ],
        name="condense",
    )(
        block_map,
        inv_interior,
        coupling,
        boundary_stiff,
        mass_interior.reshape(subs, 1, inner),
        mass_boundary.reshape(subs, 1, edge),
    )


def exchange_kernel(
    a1, b1, ma1, mb1, modes_t,
    a2, b2, ma2, mb2, cm, rm,
    arr_a, arr_b, arr_ma, arr_mb, pk_a, pk_b, pk_ma, pk_mb,
    a1s, a1r, b1s, b1r, ma1s, ma1r, mb1s, mb1r,
    a2s, a2r, b2s, b2r, ma2s, ma2r, mb2s, mb2r,
    m1s, m1r, m2s, m2r, chs, chr_, sbs, sbr, local,
):
    at = Place()
    row, col = at.row, at.col

    def remote(src, dst, ssem, rsem, r, c):
        return pltpu.make_async_remote_copy(
            src_ref=src, dst_ref=dst, send_sem=ssem, recv_sem=rsem,
            device_id=(r, c), device_id_type=MESH,
        )

    barrier = pltpu.get_barrier_semaphore()
    for dz, dy in ROW_OFFS[1:]:
        pl.semaphore_signal(barrier, inc=1, device_id=(at.row_at(dz, dy), col), device_id_type=MESH)
    for dx, dk in COL_OFFS[1:]:
        pl.semaphore_signal(barrier, inc=1, device_id=(row, at.col_at(dx, dk)), device_id_type=MESH)

    locals_ = [
        pltpu.make_async_copy(a1.at[row], arr_a.at[0], local.at[0]),
        pltpu.make_async_copy(b1.at[pl.ds(2 * col, 2)], arr_b.at[0], local.at[1]),
        pltpu.make_async_copy(ma1.at[row], arr_ma.at[0], local.at[2]),
        pltpu.make_async_copy(mb1.at[pl.ds(2 * col, 2)], arr_mb.at[0], local.at[3]),
        pltpu.make_async_copy(modes_t.at[:, pl.ds(0, 1024)], cm.at[0, row], local.at[4]),
        pltpu.make_async_copy(modes_t.at[:, pl.ds(1024, 1024)], cm.at[1, row], local.at[5]),
    ]
    for copy in locals_:
        copy.start()
    pl.semaphore_wait(barrier, 22)

    sends = []

    def go(copy):
        copy.start()
        sends.append(copy)
        return copy

    first = []
    for d in (1, 3, 2):
        for h in range(2):
            r = at.row_at(d, 0) if h == 0 else at.row_at(0, d)
            n = h * 3 + d - 1
            first.append(
                go(
                    remote(
                        modes_t.at[:, pl.ds(h * 1024, 1024)], cm.at[h, row],
                        m1s.at[n], m1r.at[n], r, col,
                    )
                )
            )
    def leg_a(n):
        r = at.row_at(*ROW_OFFS[n])
        go(remote(ma1.at[r], arr_ma.at[n], ma1s.at[n], ma1r.at[n], r, col))
        go(remote(a1.at[r], arr_a.at[n], a1s.at[n], a1r.at[n], r, col))

    def leg_b(n):
        c = at.col_at(*COL_OFFS[n])
        go(remote(mb1.at[pl.ds(2 * c, 2)], arr_mb.at[n], mb1s.at[n], mb1r.at[n], row, c))
        go(remote(b1.at[pl.ds(2 * c, 2)], arr_b.at[n], b1s.at[n], b1r.at[n], row, c))

    for n in range(1, 16):
        leg_a(n)
        if n < 8:
            leg_b(n)

    def wait_in(dst, rsem):
        remote(dst, dst, rsem, rsem, row, col).wait_recv()

    locals_[4].wait()
    locals_[5].wait()
    for d in (0, 1, 3, 2):
        for h in range(2):
            if d:
                back = at.row_at(4 - d, 0) if h == 0 else at.row_at(0, 4 - d)
                wait_in(cm.at[h, back], m1r.at[h * 3 + d - 1])
            else:
                back = row
            for e in (1, 3, 2):
                r = at.row_at(0, e) if h == 0 else at.row_at(e, 0)
                n = h * 12 + d * 3 + e - 1
                go(remote(cm.at[h, back], cm.at[h, back], m2s.at[n], m2r.at[n], r, col))

    lanes = lax.broadcasted_iota(I32, (8, BLK), 1)
    pk_ma[...] = jnp.zeros_like(pk_ma)
    pk_mb[...] = jnp.zeros_like(pk_mb)

    def pack_a(n, carry):
        meta = arr_ma[n]
        base = lax.rem(meta[4:5, :], 8) * 16 + 1
        for o in range(8):
            c = at.col_at(*COL_OFFS[o])
            total = jnp.zeros((BLK, BLK), BF16)
            slot = jnp.zeros((1, BLK), I32)
            for b in range(4):
                q = meta[b : b + 1, :]
                hit = lax.div(q, 16) == c
                mask = jnp.where(hit, F32(1.0), F32(0.0)).astype(BF16)
                total = total + arr_a[n, :, b * BLK : (b + 1) * BLK] * mask
                slot = slot + jnp.where(hit, base + lax.rem(q, 16), 0)
            pk_a[o, n] = total
            pk_ma[o] = pk_ma[o] + jnp.where(lanes == n, slot, 0)
        return carry

    def pack_b(n, carry):
        def each(o, inner):
            r = lax.rem(at.z + lax.div(o, 4), 4) * 4 + lax.rem(at.y + lax.rem(o, 4), 4)
            total = jnp.zeros((BLK, BLK), BF16)
            slot = jnp.zeros((1, BLK), I32)
            for h in range(2):
                meta = arr_mb[n, h]
                base = lax.rem(meta[4:5, :], 16) + 1
                for a in range(4):
                    p = meta[a : a + 1, :]
                    hit = lax.div(p, 8) == r
                    mask = jnp.where(hit, F32(1.0), F32(0.0)).astype(BF16)
                    total = total + arr_b[n, h, a * BLK : (a + 1) * BLK, :] * mask
                    slot = slot + jnp.where(hit, base + lax.rem(p, 8) * 16, 0)
            pk_b[o, n] = total
            pk_mb[o] = pk_mb[o] + jnp.where(lanes == n, slot, 0)
            return inner

        return lax.fori_loop(0, 16, each, carry)

    own_out = []

    def second_a(g):
        for n in range(4 * g, 4 * g + 4):
            if n:
                wait_in(arr_ma.at[n], ma1r.at[n])
                wait_in(arr_a.at[n], a1r.at[n])
        lax.fori_loop(4 * g, 4 * g + 4, pack_a, 0)
        for o in range(1, 8):
            c = at.col_at(*COL_OFFS[o])
            part = pl.ds(4 * g, 4)
            go(
                remote(
                    pk_a.at[o, part], a2.at[o, part],
                    a2s.at[o * 4 + g], a2r.at[o * 4 + g], row, c,
                )
            )
        keep = pltpu.make_async_copy(
            pk_a.at[0, pl.ds(4 * g, 4)], a2.at[0, pl.ds(4 * g, 4)], local.at[6 + g]
        )
        keep.start()
        own_out.append(keep)

    def second_b(g):
        for n in range(4 * g, 4 * g + 4):
            if n:
                wait_in(arr_mb.at[n], mb1r.at[n])
                wait_in(arr_b.at[n], b1r.at[n])
        lax.fori_loop(4 * g, 4 * g + 4, pack_b, 0)
        for o in range(1, 16):
            r = at.row_at(*ROW_OFFS[o])
            part = pl.ds(4 * g, 4)
            go(
                remote(
                    pk_b.at[o, part], b2.at[o, part],
                    b2s.at[o * 2 + g], b2r.at[o * 2 + g], r, col,
                )
            )
        keep = pltpu.make_async_copy(
            pk_b.at[0, pl.ds(4 * g, 4)], b2.at[0, pl.ds(4 * g, 4)], local.at[10 + g]
        )
        keep.start()
        own_out.append(keep)

    for copy in locals_[:4]:
        copy.wait()
    second_a(0)
    second_b(0)
    second_a(1)
    second_a(2)
    second_b(1)
    second_a(3)
    for o in range(1, 8):
        go(remote(pk_ma.at[o], ma2.at[o], ma2s.at[o], ma2r.at[o], row, at.col_at(*COL_OFFS[o])))
    for o in range(1, 16):
        go(remote(pk_mb.at[o], mb2.at[o], mb2s.at[o], mb2r.at[o], at.row_at(*ROW_OFFS[o]), col))
    for ref, out, n in ((pk_ma, ma2, 12), (pk_mb, mb2, 13)):
        keep = pltpu.make_async_copy(ref.at[0], out.at[0], local.at[n])
        keep.start()
        own_out.append(keep)

    for d in (0, 1, 3, 2):
        for h in range(2):
            for e in (1, 3, 2):
                if h == 0:
                    back = at.row_at(4 - d, 4 - e)
                else:
                    back = at.row_at(4 - e, 4 - d)
                n = h * 12 + d * 3 + e - 1
                wait_in(cm.at[h, back], m2r.at[n])
    lane = lax.div(at.y, 2)
    half = lax.rem(row, 2)
    on_lane = at.k == lane
    root = jnp.logical_and(on_lane, at.x == at.z)
    inner = jnp.logical_and(on_lane, at.x != at.z)
    far = (lax.rem(at.x + 4 - at.z, 4), lax.rem(at.z + 4 - at.x, 4))
    sibling = at.col_at(0, 1)

    def chain(n):
        step = at.col_at(1, 0) if n < 8 else at.col_at(3, 0)
        onward = remote(rm.at[n], rm.at[n], chs.at[n], chr_.at[n], row, step)
        across = remote(rm.at[n], rm.at[n], sbs.at[n], sbr.at[n], row, sibling)
        start = remote(cm.at[half, n], rm.at[n], chs.at[n], chr_.at[n], row, step)
        start_across = remote(cm.at[half, n], rm.at[n], sbs.at[n], sbr.at[n], row, sibling)
        forwards = jnp.logical_and(inner, far[0 if n < 8 else 1] < 3)
        return onward, across, start, start_across, forwards

    order = [n for pair in zip(range(8), range(8, 16)) for n in pair]
    for n in order:
        onward, across, start, start_across, forwards = chain(n)

        @pl.when(root)
        def _():
            start.start()
            start_across.start()

        @pl.when(inner)
        def _():
            onward.wait_recv()
            across.start()

        @pl.when(forwards)
        def _():
            onward.start()

    for n in order:
        onward, across, start, start_across, forwards = chain(n)

        @pl.when(on_lane)
        def _():
            across.wait_send()

        @pl.when(jnp.logical_not(on_lane))
        def _():
            across.wait_recv()

        @pl.when(jnp.logical_or(root, forwards))
        def _():
            onward.wait_send()

    for o in range(1, 8):
        for g in range(4):
            wait_in(a2.at[o, pl.ds(4 * g, 4)], a2r.at[o * 4 + g])
        wait_in(ma2.at[o], ma2r.at[o])
    for o in range(1, 16):
        for g in range(2):
            wait_in(b2.at[o, pl.ds(4 * g, 4)], b2r.at[o * 2 + g])
        wait_in(mb2.at[o], mb2r.at[o])
    for copy in own_out:
        copy.wait()
    for copy in sends:
        copy.wait_send()


def exchange(a1, b1, ma1, mb1, modes_t):
    edge = a1.shape[2]
    return pl.pallas_call(
        exchange_kernel,
        in_specs=[ANY] * 5,
        out_specs=[ANY] * 6,
        out_shape=[
            jax.ShapeDtypeStruct((8, 16, BLK, BLK), BF16),
            jax.ShapeDtypeStruct((16, 8, BLK, BLK), BF16),
            jax.ShapeDtypeStruct((8, 8, BLK), I32),
            jax.ShapeDtypeStruct((16, 8, BLK), I32),
            jax.ShapeDtypeStruct((2, 16, 64, 1024), BF16),
            jax.ShapeDtypeStruct((16, 64, 1024), BF16),
        ],
        scratch_shapes=[
            pltpu.VMEM((16, BLK, edge), BF16),
            pltpu.VMEM((8, 2, edge, BLK), BF16),
            pltpu.VMEM((16, 8, BLK), I32),
            pltpu.VMEM((8, 2, 8, BLK), I32),
            pltpu.VMEM((8, 16, BLK, BLK), BF16),
            pltpu.VMEM((16, 8, BLK, BLK), BF16),
            pltpu.VMEM((8, 8, BLK), I32),
            pltpu.VMEM((16, 8, BLK), I32),
            DMA((16,)), DMA((16,)), DMA((8,)), DMA((8,)),
            DMA((16,)), DMA((16,)), DMA((8,)), DMA((8,)),
            DMA((32,)), DMA((32,)), DMA((32,)), DMA((32,)),
            DMA((8,)), DMA((8,)), DMA((16,)), DMA((16,)),
            DMA((6,)), DMA((6,)), DMA((24,)), DMA((24,)),
            DMA((16,)), DMA((16,)), DMA((16,)), DMA((16,)),
            DMA((16,)),
        ],
        compiler_params=pltpu.CompilerParams(collective_id=0, has_side_effects=True),
        name="exchange",
    )(a1, b1, ma1, mb1, modes_t)


def assemble_kernel(
    a2, b2, ma2, mb2, cm, rm,
    stiff_out, mass_out, part_out, diag_out,
    va, vb, sa, sb, vcm, vrm, acc, tile, mass_tile, image, part, sems,
):
    at = Place()
    half = lax.rem(at.row, 2)
    holder = at.col == lax.div(at.row, 2)
    copies = [
        pltpu.make_async_copy(ma2, sa, sems.at[0]),
        pltpu.make_async_copy(a2, va, sems.at[1]),
        pltpu.make_async_copy(cm, vcm, sems.at[2]),
        pltpu.make_async_copy(mb2, sb, sems.at[3]),
        pltpu.make_async_copy(b2, vb, sems.at[4]),
    ]
    for copy in copies:
        copy.start()

    @pl.when(holder)
    def _():
        pltpu.make_async_copy(cm.at[half], vrm, sems.at[5]).start()

    @pl.when(jnp.logical_not(holder))
    def _():
        pltpu.make_async_copy(rm, vrm, sems.at[5]).start()

    def clear():
        def one(n, carry):
            acc[n] = jnp.zeros((BLK, BLK), F32)
            return carry

        lax.fori_loop(0, 128, one, 0)

    def gather(blocks, slots, senders, each):
        def one(n, carry):
            o, k = lax.div(n, each), lax.rem(n, each)
            slot = slots[o, 0, k]

            @pl.when(slot > 0)
            def _():
                acc[slot - 1] = acc[slot - 1] + blocks[o, k].astype(F32)

            return carry

        lax.fori_loop(0, senders * each, one, 0)

    def round_to(out):
        def one(p, carry):
            rows = pl.ds(pl.multiple_of(p * BLK, BLK), BLK)
            for q in range(16):
                out[rows, q * BLK : (q + 1) * BLK] = acc[p * 16 + q].astype(BF16)
            return carry

        lax.fori_loop(0, 8, one, 0)

    def products(source, offset):
        width = vcm.shape[3]
        for m in range(4):
            total = None
            for h in range(2):
                modes = vcm[h, 4 * m : 4 * m + 4].reshape(256, width)
                add = lax.dot_general(
                    source[:, h * width : (h + 1) * width], modes,
                    (((1,), (1,)), ((), ())), preferred_element_type=F32,
                )
                total = add if total is None else total + add
            image[...] = total.astype(BF16)
            left = vrm[...].reshape(1024, width)
            part[:, offset + m * 256 : offset + (m + 1) * 256] = jnp.dot(
                left, image[...], preferred_element_type=F32
            ).astype(BF16)

    clear()
    copies[0].wait()
    copies[1].wait()
    gather(va, sa, 8, 16)
    round_to(tile)
    out_stiff = pltpu.make_async_copy(tile, stiff_out, sems.at[6])
    out_stiff.start()
    copies[2].wait()
    pltpu.make_async_copy(rm, vrm, sems.at[5]).wait()
    products(tile, 0)
    out_first = pltpu.make_async_copy(
        part.at[:, pl.ds(0, 1024)], part_out.at[:, pl.ds(0, 1024)], sems.at[8]
    )
    out_first.start()
    clear()
    copies[3].wait()
    copies[4].wait()
    gather(vb, sb, 16, 8)
    round_to(mass_tile)
    out_stiff.wait()
    products(mass_tile, 1024)
    row_ids = lax.broadcasted_iota(I32, (BLK, BLK), 0)
    col_ids = lax.broadcasted_iota(I32, (BLK, BLK), 1)
    same = row_ids == col_ids

    @pl.when(holder)
    def _():
        for p in range(8):
            block = acc[p * 17 + half * 8]
            line = jnp.sum(jnp.where(same, block, F32(0.0)), axis=0, keepdims=True)
            diag_out[p] = jnp.broadcast_to(line, (8, BLK))
            rest = jnp.where(same, F32(0.0), block).astype(BF16)
            mass_tile[p * BLK : (p + 1) * BLK, pl.ds(pl.multiple_of(half * 1024 + p * BLK, BLK), BLK)] = rest

    @pl.when(jnp.logical_not(holder))
    def _():
        diag_out[...] = jnp.zeros_like(diag_out)

    out_mass = pltpu.make_async_copy(mass_tile, mass_out, sems.at[7])
    out_mass.start()
    out_second = pltpu.make_async_copy(
        part.at[:, pl.ds(1024, 1024)], part_out.at[:, pl.ds(1024, 1024)], sems.at[9]
    )
    out_second.start()
    out_first.wait()
    out_mass.wait()
    out_second.wait()


def assemble(a2, b2, ma2, mb2, cm, rm):
    return pl.pallas_call(
        assemble_kernel,
        in_specs=[ANY] * 6,
        out_specs=[ANY, ANY, ANY, VMEM],
        out_shape=[
            jax.ShapeDtypeStruct((1024, 2048), BF16),
            jax.ShapeDtypeStruct((1024, 2048), BF16),
            jax.ShapeDtypeStruct((1024, 2048), BF16),
            jax.ShapeDtypeStruct((8, 8, BLK), F32),
        ],
        scratch_shapes=[
            pltpu.VMEM((8, 16, BLK, BLK), BF16),
            pltpu.VMEM((16, 8, BLK, BLK), BF16),
            pltpu.SMEM((8, 8, BLK), I32),
            pltpu.SMEM((16, 8, BLK), I32),
            pltpu.VMEM((2, 16, 64, 1024), BF16),
            pltpu.VMEM((16, 64, 1024), BF16),
            pltpu.VMEM((128, BLK, BLK), F32),
            pltpu.VMEM((1024, 2048), BF16),
            pltpu.VMEM((1024, 2048), BF16),
            pltpu.VMEM((1024, 256), BF16),
            pltpu.VMEM((1024, 2048), BF16),
            DMA((10,)),
        ],
        compiler_params=pltpu.CompilerParams(vmem_limit_bytes=60 * 1024 * 1024),
        name="assemble",
    )(a2, b2, ma2, mb2, cm, rm)


def reduce_kernel(
    part, diag,
    stiff_out, mass_out, diag_out,
    own, other, sum_near, arr_row, sum_row, arr_x, send_last, arr_last,
    ns, nr, rs, rr, xs, xr, ls, lr, ds, dr, local,
):
    at = Place()
    row, col = at.row, at.col

    def remote(src, dst, ssem, rsem, r, c):
        return pltpu.make_async_remote_copy(
            src_ref=src, dst_ref=dst, send_sem=ssem, recv_sem=rsem,
            device_id=(r, c), device_id_type=MESH,
        )

    barrier = pltpu.get_barrier_semaphore()
    for dz, dy in ROW_OFFS[1:]:
        pl.semaphore_signal(barrier, inc=1, device_id=(at.row_at(dz, dy), col), device_id_type=MESH)
    for dx, dk in COL_OFFS[1:]:
        pl.semaphore_signal(barrier, inc=1, device_id=(row, at.col_at(dx, dk)), device_id_type=MESH)
    sibling = at.col_at(0, 1)
    mine = pl.ds(pl.multiple_of(at.k * 1024, 1024), 1024)
    theirs = pl.ds(pl.multiple_of((1 - at.k) * 1024, 1024), 1024)
    load = pltpu.make_async_copy(part.at[:, mine], own, local.at[0])
    load.start()
    pl.semaphore_wait(barrier, 22)
    near = remote(part.at[:, theirs], other, ns.at[0], nr.at[0], row, sibling)
    near.start()
    holder = col == lax.div(row, 2)

    def diag_copy(o):
        c = at.col_at(*COL_OFFS[o])
        return remote(diag.at[c], diag_out, ds.at[o], dr.at[0], row, c)

    @pl.when(holder)
    def _():
        for o in range(1, 8):
            diag_copy(o).start()
        keep = pltpu.make_async_copy(diag.at[col], diag_out, local.at[1])
        keep.start()
        keep.wait()

    load.wait()
    near.wait_recv()

    def add_near(n, carry):
        rows = pl.ds(pl.multiple_of(n * 64, 64), 64)
        sum_near[n] = (own[rows, :].astype(F32) + other[rows, :].astype(F32)).astype(BF16)
        return carry

    lax.fori_loop(0, 16, add_near, 0)
    row_sends = []
    for o in range(1, 16):
        r = at.row_at(*ROW_OFFS[o])
        copy = remote(sum_near.at[r], arr_row.at[o], rs.at[o], rr.at[o], r, col)
        copy.start()
        row_sends.append(copy)
    for copy in row_sends:
        copy.wait_recv()
    for n in range(4):
        lines = slice(n * 16, (n + 1) * 16)
        total = sum_near[row, lines, :].astype(F32)
        for o in range(1, 16):
            total = total + arr_row[o, lines, :].astype(F32)
        sum_row[n] = total.astype(BF16)
    x_sends = []
    for d in range(1, 4):
        xx = lax.rem(at.x + d, 4)
        copy = remote(
            sum_row.at[xx], arr_x.at[d], xs.at[d], xr.at[d], row, at.col_at(d, 0)
        )
        copy.start()
        x_sends.append(copy)
    for copy in x_sends:
        copy.wait_recv()
    total = sum_row[at.x].astype(F32)
    for d in range(1, 4):
        total = total + arr_x[d].astype(F32)
    send_last[0] = total[0:8, :]
    send_last[1] = total[8:16, :]
    last = remote(send_last.at[1 - at.k], arr_last, ls.at[0], lr.at[0], row, sibling)
    last.start()
    last.wait_recv()
    kept = send_last[at.k]
    got = arr_last[...]
    first = at.k == 0
    stiff_out[...] = jnp.where(first, kept, got)
    mass_out[...] = jnp.where(first, got, kept)

    @pl.when(jnp.logical_not(holder))
    def _():
        diag_copy(0).wait_recv()

    @pl.when(holder)
    def _():
        for o in range(1, 8):
            diag_copy(o).wait_send()

    near.wait_send()
    for copy in row_sends + x_sends + [last]:
        copy.wait_send()


def reduce_parts(part, diag):
    return pl.pallas_call(
        reduce_kernel,
        in_specs=[ANY, VMEM],
        out_specs=[VMEM, VMEM, VMEM],
        out_shape=[
            jax.ShapeDtypeStruct((8, 1024), F32),
            jax.ShapeDtypeStruct((8, 1024), F32),
            jax.ShapeDtypeStruct((8, BLK), F32),
        ],
        scratch_shapes=[
            pltpu.VMEM((1024, 1024), BF16),
            pltpu.VMEM((1024, 1024), BF16),
            pltpu.VMEM((16, 64, 1024), BF16),
            pltpu.VMEM((16, 64, 1024), BF16),
            pltpu.VMEM((4, 16, 1024), BF16),
            pltpu.VMEM((4, 16, 1024), BF16),
            pltpu.VMEM((2, 8, 1024), F32),
            pltpu.VMEM((8, 1024), F32),
            DMA((1,)), DMA((1,)), DMA((16,)), DMA((16,)), DMA((4,)), DMA((4,)),
            DMA((1,)), DMA((1,)), DMA((8,)), DMA((1,)), DMA((2,)),
        ],
        compiler_params=pltpu.CompilerParams(collective_id=1, has_side_effects=True),
        name="reduce",
    )(part, diag)


def body(inv_interior, coupling, boundary_stiff, mass_interior, mass_boundary, block_map, modes):
    a1, b1, ma1, mb1 = condense(
        inv_interior, coupling, boundary_stiff, mass_interior, mass_boundary, block_map
    )
    moved = exchange(a1, b1, ma1, mb1, modes.T)
    stiff_tile, mass_tile, part, diag = assemble(*moved)
    stiff, mass, diagonal = reduce_parts(part, diag)
    return stiff_tile, mass_tile, stiff, mass, diagonal[0]


def solution(mesh):
    both = ("row", "col")
    return jax.shard_map(
        body,
        mesh=mesh,
        in_specs=(
            P(both, None, None),
            P(both, None, None),
            P(both, None, None),
            P(both, None),
            P(both, None),
            P(both, None),
            P("col", "row"),
        ),
        out_specs=(
            P("row", "col"),
            P("row", "col"),
            P(both, None),
            P(both, None),
            P(both),
        ),
        check_vma=False,
    )
```

time: 444 us -> 340 us (0.77); the launches traced: 436 us -> 339 us
  Pallas kernels: 0 us -> 332 us
  waiting for transfers between devices: 124 us -> 0 us
  other arithmetic: 90.1 us -> 0 us
  local copies, waits for them, and re-layouts: 69.9 us -> 6.57 us
  matrix products: 52.3 us -> 0 us
  blocking collectives: 46.9 us -> 0 us
  starting transfers between devices: 38.7 us -> 0 us
  between operations: 14.4 us -> 0.66 us
    pallas_call x0 -> x4, Pallas kernels: none -> 332 us  [the longest x1 150 us: reduce_parts(): pl.pallas_call(reduce_kernel, in_specs=[ANY, VMEM], out_specs=[VMEM, VMEM...]
    all_gather x1 -> x0, waiting for transfers between devices: 115 us -> none  [body(): col_modes = lax.all_gather(modes, ROW, axis=1, tiled=True)]
    dot_general x15 -> x0, matrix products: 52.3 us -> none  [the longest x1 15.8 us: body(): jnp.dot(left_modes.T, right_side, precision=lax.Precision.HIGHEST, prefer...]
    all_to_all x2 -> x0, blocking collectives: 46.9 us -> none  [the longest x1 38.9 us: summed_rows(): lax.all_to_all(nearer.astype(jnp.bfloat16), far, split_axis=0, concat_axi...]
    scatter-add x1 -> x0, other arithmetic: 37 us -> none  [body(): jax.ops.segment_sum(arrived, jnp.maximum(arrived_slots, 0), num_segments=...]
    convert_element_type x4 -> x0, other arithmetic: 28 us -> none  [the longest x1 11.3 us: body(): arrived, arrived_slots = (lax.all_to_all(outgoing.astype(jnp.bfloat16), R...]
    all_to_all x3 -> x0, starting transfers between devices: 27.2 us -> none  [the longest x1 11.5 us: body(): lax.all_to_all(targets, ROW_COL, split_axis=0, concat_axis=0, tiled=True)]
    slice x4 -> x0, local copies, waits for them, and re-layouts: 15.2 us -> none  [the longest x2 11.8 us: body(): mass_tile = full_pair[1]]
  transfers between devices with their start and end apart: 6 -> 0, of which waited for: 2 -> 0; matrix products, arithmetic and copies ran while one was open for 42% -> 0% of each run, Pallas kernels for 0% -> 0%
where the time goes in v1:
time: 340 us; the launch traced here: 339 us
  Pallas kernels  332 us (98%)
  local copies, waits for them, and re-layouts  6.57 us (2%)
    pallas_call x1, Pallas kernels, reduce_parts(): pl.pallas_call(reduce_kernel, in_specs=[ANY, VMEM], out_specs=[VMEM, VMEM...  150 us
    pallas_call x1, Pallas kernels, exchange(): pl.pallas_call(exchange_kernel, in_specs=[ANY] * 5, out_specs=[ANY] * 6,...  130 us
    pallas_call x1, Pallas kernels, assemble(): pl.pallas_call(assemble_kernel, in_specs=[ANY] * 6, out_specs=[ANY, ANY,...  38.2 us
    pallas_call x1, Pallas kernels, condense(): pl.pallas_call(condense_kernel, grid_spec=pltpu.PrefetchScalarGridSpec(nu...  14.2 us

profile of v1, /device:TPU:1, one launch (start us, length us, event | category | flops | bytes accessed | tf_op | source)
XLA Modules:
  0.0 339.1 jit_solution(16110149846430954798)
XLA Ops:
  0.6 1.3 reshape.17.mb_ref
  1.9 1.3 reshape.16.mi_ref
  3.3 14.2 %condense.1 = (bf16[16,128,512]{2,1,0:T(8,128)(2,1)}, bf16[16,512,128]{2,1,0:T(8,128)(2,1)}, s32[16,8,128]{2,1,0:T(8,128)}, s32[16,8,128]{2,1,0:T(8,128)}) custom-call(s32[4,4]{1,0:T(4,128)} %map_ref.1, bf16[4,1024,1024]{2,1,0:T(8,128)(2,1)} %inv_ref.1, bf16[4,1024,512]{2,1,0:T(8,128)(2,1)} %couple_ref.1, bf16[4,512,512]{2,1,0:T(8,128)(2,1)} %stiff_ref.1, ...), custom_call_target="tpu_custom_call" | custom-call | tf_op jit(solution)/shard_map/condense/pallas_call | solution.py:73
  17.5 129.8 %exchange.1 = (bf16[8,16,128,128]{3,2,1,0:T(8,128)(2,1)}, bf16[16,8,128,128]{3,2,1,0:T(8,128)(2,1)}, s32[8,8,128]{2,1,0:T(8,128)}, s32[16,8,128]{2,1,0:T(8,128)}...) custom-call(bf16[16,128,512]{2,1,0:T(8,128)(2,1)} %get-tuple-element.22.a1, ...), custom_call_target="tpu_custom_call" | custom-call | tf_op jit(solution)/shard_map/exchange/pallas_call | solution.py:373
  147.3 38.2 %assemble.1 = (bf16[1024,2048]{1,0:T(8,128)(2,1)}, bf16[1024,2048]{1,0:T(8,128)(2,1)}, bf16[1024,2048]{1,0:T(8,128)(2,1)}, f32[8,8,128]{2,1,0:T(8,128)}) custom-call(bf16[8,16,128,128]{3,2,1,0:T(8,128)(2,1)} %get-tuple-element.26.a2, bf16[16,8,128,128]{3,2,1,0:T(8,128)(2,1)} %get-tuple-element.27.b2, s32[8,8,128]{2,1,0:T(8,128)} %get-tuple-element.28.ma2, ...), custom_call_target="tpu_custom_call" | custom-call | tf_op jit(solution)/shard_map/assemble/pallas_call | solution.py:529
  185.5 149.7 %reduce.1 = (f32[8,1024]{1,0:T(8,128)}, f32[8,1024]{1,0:T(8,128)}, f32[8,128]{1,0:T(8,128)}) custom-call(bf16[1024,2048]{1,0:T(8,128)(2,1)} %get-tuple-element.34.part, f32[8,8,128]{2,1,0:T(8,128)} %get-tuple-element.35.diag), custom_call_target="tpu_custom_call" | custom-call | tf_op jit(solution)/shard_map/reduce/pallas_call | solution.py:662
  335.2 1.2 slice_bitcast_fusion
  336.3 1.4 copy.14
  337.7 1.4 copy.15

commit v2 on v1

v2 whole, which is shorter than its diff:
```python
import functools

import jax
import jax.numpy as jnp
from jax import lax
from jax.experimental import pallas as pl
from jax.experimental.pallas import tpu as pltpu
from jax.sharding import PartitionSpec as P

MESH = pl.DeviceIdType.MESH
BLK = 128
F32 = jnp.float32
BF16 = jnp.bfloat16
I32 = jnp.int32
ANY = pl.BlockSpec(memory_space=pl.ANY)
VMEM = pl.BlockSpec(memory_space=pltpu.VMEM)
DMA = pltpu.SemaphoreType.DMA
ROW_OFFS = [(dz, dy) for dz in range(4) for dy in range(4)]
COL_OFFS = [(dx, dk) for dx in range(4) for dk in range(2)]


class Place:
    def __init__(self):
        self.row = lax.axis_index("row")
        self.col = lax.axis_index("col")
        self.z, self.y = lax.div(self.row, 4), lax.rem(self.row, 4)
        self.x, self.k = lax.div(self.col, 2), lax.rem(self.col, 2)

    def row_at(self, dz, dy):
        return lax.rem(self.z + dz, 4) * 4 + lax.rem(self.y + dy, 4)

    def col_at(self, dx, dk):
        return lax.rem(self.x + dx, 4) * 2 + lax.rem(self.k + dk, 2)


THIRDS = ((0, 6), (6, 4), (10, 6))


def exchange_kernel(
    map_ref, inv, couple, stiff, mi_ref, mb_ref, modes_t,
    a2, b2, ma2, mb2, cm, rm,
    v_inv, v_couple, v_stiff, nat_a, nat_b, st_a, st_b, st_ma, st_mb,
    arr_a, arr_b, arr_ma, arr_mb, pk_a, pk_b, pk_ma, pk_mb,
    lds, a1s, a1r, b1s, b1r, ma1s, ma1r, mb1s, mb1r,
    a2s, a2r, b2s, b2r, ma2s, ma2r, mb2s, mb2r,
    m1s, m1r, m2s, m2r, rms, rmr, sbs, sbr, local,
):
    at = Place()
    row, col = at.row, at.col

    def remote(src, dst, ssem, rsem, r, c):
        return pltpu.make_async_remote_copy(
            src_ref=src, dst_ref=dst, send_sem=ssem, recv_sem=rsem,
            device_id=(r, c), device_id_type=MESH,
        )

    barrier = pltpu.get_barrier_semaphore()
    for dz, dy in ROW_OFFS[1:]:
        pl.semaphore_signal(barrier, inc=1, device_id=(at.row_at(dz, dy), col), device_id_type=MESH)
    for dx, dk in COL_OFFS[1:]:
        pl.semaphore_signal(barrier, inc=1, device_id=(row, at.col_at(dx, dk)), device_id_type=MESH)

    def loads(s):
        return [
            pltpu.make_async_copy(inv.at[s], v_inv.at[s], lds.at[0, s]),
            pltpu.make_async_copy(couple.at[s], v_couple.at[s], lds.at[1, s]),
            pltpu.make_async_copy(stiff.at[s], v_stiff.at[s], lds.at[2, s]),
        ]

    for s in range(4):
        for copy in loads(s):
            copy.start()
    own_modes = [
        pltpu.make_async_copy(modes_t.at[:, pl.ds(h * 1024, 1024)], cm.at[h, row], local.at[h])
        for h in range(2)
    ]
    for copy in own_modes:
        copy.start()

    sends = []

    def go(copy):
        copy.start()
        sends.append(copy)

    def wait_in(dst, rsem):
        remote(dst, dst, rsem, rsem, row, col).wait_recv()

    def condense(s, carry):
        for copy in loads(s):
            copy.wait()
        pair = v_couple[s]
        static = (-jnp.dot(v_inv[s], pair, preferred_element_type=F32)).astype(BF16)
        stiffness = v_stiff[s].astype(F32) + lax.dot_general(
            pair, static, (((0,), (0,)), ((), ())), preferred_element_type=F32
        )
        stiffness = stiffness.astype(BF16)
        for a in range(4):
            nat_a[s * 4 + a] = stiffness[a * BLK : (a + 1) * BLK, :]
        static_t = static.T
        weighted_t = (static_t.astype(F32) * mi_ref[pl.ds(s, 1), :]).astype(BF16)
        mass = lax.dot_general(
            static_t, weighted_t, (((1,), (1,)), ((), ())), preferred_element_type=F32
        )
        width = mass.shape[0]
        row_ids = lax.broadcasted_iota(I32, (width, width), 0)
        col_ids = lax.broadcasted_iota(I32, (width, width), 1)
        mass = mass + jnp.where(row_ids == col_ids, mb_ref[pl.ds(s, 1), :], F32(0.0))
        mass = mass.astype(BF16)
        for b in range(4):
            nat_b[s * 4 + b] = mass[:, b * BLK : (b + 1) * BLK]
        return carry

    lax.fori_loop(0, 1, condense, 0)
    pl.semaphore_wait(barrier, 22)
    for d in (1, 3, 2):
        for h in range(2):
            r = at.row_at(d, 0) if h == 0 else at.row_at(0, d)
            n = h * 3 + d - 1
            go(
                remote(
                    modes_t.at[:, pl.ds(h * 1024, 1024)], cm.at[h, row],
                    m1s.at[n], m1r.at[n], r, col,
                )
            )
    lax.fori_loop(1, 3, condense, 0)
    for copy in own_modes:
        copy.wait()
    for d in (0, 1, 3, 2):
        for h in range(2):
            if d:
                back = at.row_at(4 - d, 0) if h == 0 else at.row_at(0, 4 - d)
                wait_in(cm.at[h, back], m1r.at[h * 3 + d - 1])
            else:
                back = row
            for e in (1, 3, 2):
                r = at.row_at(0, e) if h == 0 else at.row_at(e, 0)
                n = h * 12 + d * 3 + e - 1
                go(remote(cm.at[h, back], cm.at[h, back], m2s.at[n], m2r.at[n], r, col))
    lax.fori_loop(3, 4, condense, 0)

    lines = lax.broadcasted_iota(I32, (8, BLK), 0)

    def find(tile_row):
        found = jnp.int32(0)
        for n in range(16):
            found = jnp.where(lax.div(map_ref[n // 4, n % 4], 8) == tile_row, n, found)
        sub = lax.div(found, 4)
        table = jnp.full((8, BLK), map_ref[sub, lax.rem(found, 4)], I32)
        for a in range(4):
            table = jnp.where(lines == a, map_ref[sub, a], table)
        return found, table

    def stage_a(o, carry):
        r = lax.rem(at.z + lax.div(o, 4), 4) * 4 + lax.rem(at.y + lax.rem(o, 4), 4)
        found, table = find(r)
        st_a[o] = nat_a[found]
        st_ma[o] = table
        return carry

    def stage_b(o, carry):
        n, h = lax.div(o, 2), lax.rem(o, 2)
        c = lax.rem(at.x + lax.div(n, 2), 4) * 2 + lax.rem(at.k + lax.rem(n, 2), 2)
        found, table = find(2 * c + h)
        st_b[n, h] = nat_b[found]
        st_mb[n, h] = table
        return carry

    lax.fori_loop(0, 16, stage_b, 0)
    for n in range(1, 8):
        c = at.col_at(*COL_OFFS[n])
        go(remote(st_mb.at[n], arr_mb.at[n], mb1s.at[n], mb1r.at[n], row, c))
        go(remote(st_b.at[n], arr_b.at[n], b1s.at[n], b1r.at[n], row, c))
    lax.fori_loop(0, 16, stage_a, 0)
    for n in range(1, 16):
        r = at.row_at(*ROW_OFFS[n])
        go(remote(st_ma.at[n], arr_ma.at[n], ma1s.at[n], ma1r.at[n], r, col))
        go(remote(st_a.at[n], arr_a.at[n], a1s.at[n], a1r.at[n], r, col))
    arr_a[0] = st_a[0]
    arr_ma[0] = st_ma[0]
    arr_b[0] = st_b[0]
    arr_mb[0] = st_mb[0]
    pk_ma[...] = jnp.zeros_like(pk_ma)
    pk_mb[...] = jnp.zeros_like(pk_mb)
    lanes = lax.broadcasted_iota(I32, (8, BLK), 1)

    for d in (0, 1, 3, 2):
        for h in range(2):
            for e in (1, 3, 2):
                back = at.row_at(4 - d, 4 - e) if h == 0 else at.row_at(4 - e, 4 - d)
                wait_in(cm.at[h, back], m2r.at[h * 12 + d * 3 + e - 1])
    half = lax.rem(row, 2)
    on_lane = at.k == lax.div(at.y, 2)
    place = lax.rem(at.x + 4 - at.z, 4)
    root = jnp.logical_and(on_lane, place == 0)
    inner = jnp.logical_and(on_lane, place > 0)
    sibling = at.col_at(0, 1)

    def third(t):
        return pl.ds(THIRDS[t][0], THIRDS[t][1])

    def out_third(t):
        return remote(
            cm.at[half, third(t)], rm.at[third(t)], rms.at[t], rmr.at[t], row, at.col_at(t + 1, 0)
        )

    def root_across(t):
        return remote(
            cm.at[half, third(t)], rm.at[third(t)], sbs.at[t], sbr.at[t], row, sibling
        )

    def across(t):
        return remote(rm.at[third(t)], rm.at[third(t)], sbs.at[t], sbr.at[t], row, sibling)

    def onward(t, u):
        return remote(
            rm.at[third(t)], rm.at[third(t)], rms.at[u], rmr.at[t], row, at.col_at(u + 4 - t, 0)
        )

    @pl.when(root)
    def _():
        for t in range(3):
            out_third(t).start()
            root_across(t).start()

    def pack_a(n, carry):
        meta = arr_ma[n]
        base = lax.rem(meta[4:5, :], 8) * 16 + 1
        for o in range(8):
            c = at.col_at(*COL_OFFS[o])
            total = jnp.zeros((BLK, BLK), BF16)
            slot = jnp.zeros((1, BLK), I32)
            for b in range(4):
                q = meta[b : b + 1, :]
                hit = lax.div(q, 16) == c
                mask = jnp.where(hit, F32(1.0), F32(0.0)).astype(BF16)
                total = total + arr_a[n, :, b * BLK : (b + 1) * BLK] * mask
                slot = jnp.where(hit, base + lax.rem(q, 16), slot)
            pk_a[o, n] = total
            pk_ma[o] = pk_ma[o] + jnp.where(lanes == n, slot, 0)
        return carry

    def pack_b(n, carry):
        def each(o, inside):
            r = lax.rem(at.z + lax.div(o, 4), 4) * 4 + lax.rem(at.y + lax.rem(o, 4), 4)
            total = jnp.zeros((BLK, BLK), BF16)
            slot = jnp.zeros((1, BLK), I32)
            for h in range(2):
                meta = arr_mb[n, h]
                base = lax.rem(meta[4:5, :], 16) + 1
                for a in range(4):
                    p = meta[a : a + 1, :]
                    hit = lax.div(p, 8) == r
                    mask = jnp.where(hit, F32(1.0), F32(0.0)).astype(BF16)
                    total = total + arr_b[n, h, a * BLK : (a + 1) * BLK, :] * mask
                    slot = jnp.where(hit, base + lax.rem(p, 8) * 16, slot)
            pk_b[o, n] = total
            pk_mb[o] = pk_mb[o] + jnp.where(lanes == n, slot, 0)
            return inside

        return lax.fori_loop(0, 16, each, carry)

    own_out = []

    def keep(src, dst, n):
        copy = pltpu.make_async_copy(src, dst, local.at[n])
        copy.start()
        own_out.append(copy)

    def second_a(g):
        part = pl.ds(4 * g, 4)
        for n in range(4 * g, 4 * g + 4):
            if n:
                wait_in(arr_ma.at[n], ma1r.at[n])
                wait_in(arr_a.at[n], a1r.at[n])
        lax.fori_loop(4 * g, 4 * g + 4, pack_a, 0)
        for o in range(1, 8):
            n = o * 4 + g
            go(
                remote(
                    pk_a.at[o, part], a2.at[o, part], a2s.at[n], a2r.at[n],
                    row, at.col_at(*COL_OFFS[o]),
                )
            )
        keep(pk_a.at[0, part], a2.at[0, part], 2 + g)

    def second_b(g):
        part = pl.ds(4 * g, 4)
        for n in range(4 * g, 4 * g + 4):
            if n:
                wait_in(arr_mb.at[n], mb1r.at[n])
                wait_in(arr_b.at[n], b1r.at[n])
        lax.fori_loop(4 * g, 4 * g + 4, pack_b, 0)
        for o in range(1, 16):
            n = o * 2 + g
            go(
                remote(
                    pk_b.at[o, part], b2.at[o, part], b2s.at[n], b2r.at[n],
                    at.row_at(*ROW_OFFS[o]), col,
                )
            )
        keep(pk_b.at[0, part], b2.at[0, part], 6 + g)

    second_a(0)
    second_b(0)
    second_a(1)
    second_b(1)
    for o in range(1, 16):
        go(remote(pk_mb.at[o], mb2.at[o], mb2s.at[o], mb2r.at[o], at.row_at(*ROW_OFFS[o]), col))
    for t in range(3):

        @pl.when(jnp.logical_and(inner, place == t + 1))
        def _():
            wait_in(rm.at[third(t)], rmr.at[t])
            for u in range(3):
                if u != t:
                    onward(t, u).start()
            across(t).start()

    second_a(2)
    second_a(3)
    for o in range(1, 8):
        go(remote(pk_ma.at[o], ma2.at[o], ma2s.at[o], ma2r.at[o], row, at.col_at(*COL_OFFS[o])))
    keep(pk_ma.at[0], ma2.at[0], 8)
    keep(pk_mb.at[0], mb2.at[0], 9)
    for t in range(3):

        @pl.when(jnp.logical_and(inner, place != t + 1))
        def _():
            wait_in(rm.at[third(t)], rmr.at[t])
            across(t).start()

    for o in range(1, 8):
        for g in range(4):
            wait_in(a2.at[o, pl.ds(4 * g, 4)], a2r.at[o * 4 + g])
        wait_in(ma2.at[o], ma2r.at[o])
    for o in range(1, 16):
        for g in range(2):
            wait_in(b2.at[o, pl.ds(4 * g, 4)], b2r.at[o * 2 + g])
        wait_in(mb2.at[o], mb2r.at[o])
    for copy in own_out:
        copy.wait()
    for t in range(3):

        @pl.when(root)
        def _():
            out_third(t).wait_send()

        @pl.when(on_lane)
        def _():
            across(t).wait_send()

        @pl.when(jnp.logical_not(on_lane))
        def _():
            across(t).wait_recv()

        @pl.when(jnp.logical_and(inner, place == t + 1))
        def _():
            for u in range(3):
                if u != t:
                    onward(t, u).wait_send()

    for copy in sends:
        copy.wait_send()


def exchange(block_map, inv_interior, coupling, boundary_stiff, mass_interior, mass_boundary, modes_t):
    subs, inside, edge = coupling.shape
    return pl.pallas_call(
        exchange_kernel,
        in_specs=[pl.BlockSpec(memory_space=pltpu.SMEM), ANY, ANY, ANY, VMEM, VMEM, ANY],
        out_specs=[ANY] * 6,
        out_shape=[
            jax.ShapeDtypeStruct((8, 16, BLK, BLK), BF16),
            jax.ShapeDtypeStruct((16, 8, BLK, BLK), BF16),
            jax.ShapeDtypeStruct((8, 8, BLK), I32),
            jax.ShapeDtypeStruct((16, 8, BLK), I32),
            jax.ShapeDtypeStruct((2, 16, 64, 1024), BF16),
            jax.ShapeDtypeStruct((16, 64, 1024), BF16),
        ],
        scratch_shapes=[
            pltpu.VMEM((subs, inside, inside), BF16),
            pltpu.VMEM((subs, inside, edge), BF16),
            pltpu.VMEM((subs, edge, edge), BF16),
            pltpu.VMEM((16, BLK, edge), BF16),
            pltpu.VMEM((16, edge, BLK), BF16),
            pltpu.VMEM((16, BLK, edge), BF16),
            pltpu.VMEM((8, 2, edge, BLK), BF16),
            pltpu.VMEM((16, 8, BLK), I32),
            pltpu.VMEM((8, 2, 8, BLK), I32),
            pltpu.VMEM((16, BLK, edge), BF16),
            pltpu.VMEM((8, 2, edge, BLK), BF16),
            pltpu.VMEM((16, 8, BLK), I32),
            pltpu.VMEM((8, 2, 8, BLK), I32),
            pltpu.VMEM((8, 16, BLK, BLK), BF16),
            pltpu.VMEM((16, 8, BLK, BLK), BF16),
            pltpu.VMEM((8, 8, BLK), I32),
            pltpu.VMEM((16, 8, BLK), I32),
            DMA((3, 4)),
            DMA((16,)), DMA((16,)), DMA((8,)), DMA((8,)),
            DMA((16,)), DMA((16,)), DMA((8,)), DMA((8,)),
            DMA((32,)), DMA((32,)), DMA((32,)), DMA((32,)),
            DMA((8,)), DMA((8,)), DMA((16,)), DMA((16,)),
            DMA((6,)), DMA((6,)), DMA((24,)), DMA((24,)),
            DMA((3,)), DMA((3,)), DMA((3,)), DMA((3,)),
            DMA((10,)),
        ],
        compiler_params=pltpu.CompilerParams(
            collective_id=0, has_side_effects=True, vmem_limit_bytes=60 * 1024 * 1024
        ),
        name="exchange",
    )(block_map, inv_interior, coupling, boundary_stiff, mass_interior, mass_boundary, modes_t)


def assemble_kernel(
    a2, b2, ma2, mb2,
    stiff_out, mass_out, diag_out,
    va, vb, sa, sb, acc, tile, mass_tile, sems,
):
    at = Place()
    half = lax.rem(at.row, 2)
    holder = at.col == lax.div(at.row, 2)
    copies = [
        pltpu.make_async_copy(ma2, sa, sems.at[0]),
        pltpu.make_async_copy(a2, va, sems.at[1]),
        pltpu.make_async_copy(mb2, sb, sems.at[2]),
        pltpu.make_async_copy(b2, vb, sems.at[3]),
    ]
    for copy in copies:
        copy.start()

    def clear(n, carry):
        acc[n] = jnp.zeros((BLK, BLK), F32)
        return carry

    def gather(base, blocks, slots, senders, each):
        def one(n, carry):
            for u in range(4):
                o, k = lax.div(n * 4, each), lax.rem(n * 4, each) + u
                slot = slots[o, 0, k] + base
                acc[slot] = acc[slot] + blocks[o, k].astype(F32)
            return carry

        lax.fori_loop(0, senders * each // 4, one, 0)

    def round_to(base, out):
        def one(p, carry):
            rows = pl.ds(pl.multiple_of(p * BLK, BLK), BLK)
            for q in range(16):
                out[rows, q * BLK : (q + 1) * BLK] = acc[base + p * 16 + q + 1].astype(BF16)
            return carry

        lax.fori_loop(0, 8, one, 0)

    lax.fori_loop(0, 258, clear, 0)
    copies[0].wait()
    copies[1].wait()
    gather(0, va, sa, 8, 16)
    round_to(0, tile)
    out_stiff = pltpu.make_async_copy(tile, stiff_out, sems.at[4])
    out_stiff.start()
    copies[2].wait()
    copies[3].wait()
    gather(129, vb, sb, 16, 8)
    round_to(129, mass_tile)
    row_ids = lax.broadcasted_iota(I32, (BLK, BLK), 0)
    col_ids = lax.broadcasted_iota(I32, (BLK, BLK), 1)
    same = row_ids == col_ids

    @pl.when(holder)
    def _():
        for p in range(8):
            block = acc[130 + p * 17 + half * 8]
            line = jnp.sum(jnp.where(same, block, F32(0.0)), axis=0, keepdims=True)
            diag_out[p] = jnp.broadcast_to(line, (8, BLK))
            rest = jnp.where(same, F32(0.0), block).astype(BF16)
            start = pl.multiple_of(half * 1024 + p * BLK, BLK)
            mass_tile[p * BLK : (p + 1) * BLK, pl.ds(start, BLK)] = rest

    @pl.when(jnp.logical_not(holder))
    def _():
        diag_out[...] = jnp.zeros_like(diag_out)

    out_mass = pltpu.make_async_copy(mass_tile, mass_out, sems.at[5])
    out_mass.start()
    out_stiff.wait()
    out_mass.wait()


def assemble(a2, b2, ma2, mb2):
    return pl.pallas_call(
        assemble_kernel,
        in_specs=[ANY] * 4,
        out_specs=[ANY, ANY, VMEM],
        out_shape=[
            jax.ShapeDtypeStruct((1024, 2048), BF16),
            jax.ShapeDtypeStruct((1024, 2048), BF16),
            jax.ShapeDtypeStruct((8, 8, BLK), F32),
        ],
        scratch_shapes=[
            pltpu.VMEM((8, 16, BLK, BLK), BF16),
            pltpu.VMEM((16, 8, BLK, BLK), BF16),
            pltpu.SMEM((8, 8, BLK), I32),
            pltpu.SMEM((16, 8, BLK), I32),
            pltpu.VMEM((258, BLK, BLK), F32),
            pltpu.VMEM((1024, 2048), BF16),
            pltpu.VMEM((1024, 2048), BF16),
            DMA((6,)),
        ],
        compiler_params=pltpu.CompilerParams(vmem_limit_bytes=60 * 1024 * 1024),
        name="assemble",
    )(a2, b2, ma2, mb2)


GROUPS = ((0, 6, "zyx"), (6, 6, "yxz"), (12, 4, "xzy"))


def reduce_kernel(
    stiff, mass, diag, cm, rm,
    stiff_out, mass_out, diag_out,
    tiles, vcm, vrm, *rest,
):
    bufs = [rest[7 * j : 7 * j + 7] for j in range(3)]
    send_last, arr_last = rest[21:23]
    ns, nr, s1, r1, s2, r2, s3, r3, ls, lr, ds, dr, local = rest[23:]
    at = Place()
    row, col = at.row, at.col
    half = lax.rem(row, 2)
    holder = col == lax.div(row, 2)
    mine = {"z": at.z, "y": at.y, "x": at.x}

    def remote(src, dst, ssem, rsem, r, c):
        return pltpu.make_async_remote_copy(
            src_ref=src, dst_ref=dst, send_sem=ssem, recv_sem=rsem,
            device_id=(r, c), device_id_type=MESH,
        )

    def away(axis, d):
        r = at.row_at(d if axis == "z" else 0, d if axis == "y" else 0)
        c = at.col_at(d if axis == "x" else 0, 0)
        return r, c, lax.rem(mine[axis] + d, 4)

    barrier = pltpu.get_barrier_semaphore()
    for d in range(1, 4):
        for axis in "zy":
            r, c, _ = away(axis, d)
            pl.semaphore_signal(barrier, inc=1, device_id=(r, c), device_id_type=MESH)
    for dx, dk in COL_OFFS[1:]:
        pl.semaphore_signal(barrier, inc=1, device_id=(row, at.col_at(dx, dk)), device_id_type=MESH)
    sibling = at.col_at(0, 1)
    loads = [
        pltpu.make_async_copy(cm, vcm, local.at[0]),
        pltpu.make_async_copy(stiff, tiles.at[0], local.at[1]),
        pltpu.make_async_copy(mass, tiles.at[1], local.at[2]),
    ]
    for copy in loads:
        copy.start()

    @pl.when(holder)
    def _():
        pltpu.make_async_copy(cm.at[half], vrm, local.at[3]).start()

    @pl.when(jnp.logical_not(holder))
    def _():
        pltpu.make_async_copy(rm, vrm, local.at[3]).start()

    for copy in loads:
        copy.wait()
    pltpu.make_async_copy(rm, vrm, local.at[3]).wait()

    @pl.when(holder)
    def _():
        row_ids = lax.broadcasted_iota(I32, (BLK, BLK), 0)
        col_ids = lax.broadcasted_iota(I32, (BLK, BLK), 1)
        for p in range(8):
            spot = (
                1,
                slice(p * BLK, (p + 1) * BLK),
                pl.ds(pl.multiple_of(half * 1024 + p * BLK, BLK), BLK),
            )
            block = tiles[spot].astype(F32)
            tiles[spot] = jnp.where(row_ids == col_ids, diag[p, 0:1, :], block).astype(BF16)

    pl.semaphore_wait(barrier, 13)

    def diag_copy(o):
        c = at.col_at(*COL_OFFS[o])
        return remote(diag.at[c], diag_out, ds.at[o], dr.at[0], row, c)

    @pl.when(holder)
    def _():
        for o in range(1, 8):
            diag_copy(o).start()
        own = pltpu.make_async_copy(diag.at[col], diag_out, local.at[4])
        own.start()
        own.wait()

    def product(which, j):
        first, count, _ = GROUPS[j]
        depth = vcm.shape[3]
        total = None
        for h in range(2):
            modes = vcm[h, first : first + count].reshape(count * 64, depth)
            add = lax.dot_general(
                tiles[which, :, h * depth : (h + 1) * depth], modes,
                (((1,), (1,)), ((), ())), preferred_element_type=F32,
            )
            total = add if total is None else total + add
        left = vrm[...].reshape(1024, depth)
        return jnp.dot(left, total.astype(BF16), preferred_element_type=F32)

    near = []
    for j in range(3):
        out_near, in_near = bufs[j][0], bufs[j][1]
        out_near[...] = product(1 - at.k, j).astype(BF16)
        copy = remote(out_near, in_near, ns.at[j], nr.at[j], row, sibling)
        copy.start()
        near.append(copy)
    sends = []

    def leg(j, level, src, dst, ssem, rsem):
        axis = GROUPS[j][2][level]
        dims = sorted(GROUPS[j][2][level:], key="zyx".index)
        spot = dims.index(axis)
        arriving = []
        for d in range(1, 4):
            r, c, place = away(axis, d)
            part = src.at[(slice(None),) * spot + (place,)]
            copy = remote(part, dst.at[d], ssem.at[j * 4 + d], rsem.at[j * 4 + d], r, c)
            copy.start()
            sends.append(copy)
            arriving.append(copy)
        return arriving, (slice(None),) * spot + (mine[axis],)

    def summed(src, own, dst, arriving):
        for copy in arriving:
            copy.wait_recv()
        total = src[own].astype(F32)
        for d in range(1, 4):
            total = total + dst[d].astype(F32)
        return total

    first_legs = []
    for j in range(3):
        _, in_near, near_sum, arr1, _, _, _ = bufs[j]
        width = GROUPS[j][1] * 64
        here = product(at.k, j)
        near[j].wait_recv()
        total = (here + in_near[...].astype(F32)).astype(BF16)
        near_sum[...] = total.reshape(4, 4, 4, 16, width)
        first_legs.append(leg(j, 0, near_sum, arr1, s1, r1))
    second_legs = []
    for j in range(3):
        _, _, near_sum, arr1, sum1, arr2, _ = bufs[j]
        arriving, own = first_legs[j]
        sum1[...] = summed(near_sum, own, arr1, arriving).astype(BF16)
        second_legs.append(leg(j, 1, sum1, arr2, s2, r2))
    third_legs = []
    for j in range(3):
        sum1, arr2, last = bufs[j][4:]
        arriving, own = second_legs[j]
        last[0] = summed(sum1, own, arr2, arriving).astype(BF16)
        third_legs.append(leg(j, 2, last.at[0], last.at[1], s3, r3))
    for j in range(3):
        last = bufs[j][6]
        arriving, own = third_legs[j]
        total = summed(last.at[0], own, last.at[1], arriving)
        cols = slice(GROUPS[j][0] * 64, (GROUPS[j][0] + GROUPS[j][1]) * 64)
        send_last[0, :, cols] = total[0:8, :]
        send_last[1, :, cols] = total[8:16, :]
    final = remote(send_last.at[1 - at.k], arr_last, ls.at[0], lr.at[0], row, sibling)
    final.start()
    final.wait_recv()
    kept = send_last[at.k]
    got = arr_last[...]
    lower = at.k == 0
    stiff_out[...] = jnp.where(lower, kept, got)
    mass_out[...] = jnp.where(lower, got, kept)

    @pl.when(jnp.logical_not(holder))
    def _():
        diag_copy(0).wait_recv()

    @pl.when(holder)
    def _():
        for o in range(1, 8):
            diag_copy(o).wait_send()

    for copy in near + sends + [final]:
        copy.wait_send()


def reduce_parts(stiff, mass, diag, cm, rm):
    scratch = [
        pltpu.VMEM((2, 1024, 2048), BF16),
        pltpu.VMEM((2, 16, 64, 1024), BF16),
        pltpu.VMEM((16, 64, 1024), BF16),
    ]
    for _, count, _ in GROUPS:
        width = count * 64
        scratch += [
            pltpu.VMEM((1024, width), BF16),
            pltpu.VMEM((1024, width), BF16),
            pltpu.VMEM((4, 4, 4, 16, width), BF16),
            pltpu.VMEM((4, 4, 4, 16, width), BF16),
            pltpu.VMEM((4, 4, 16, width), BF16),
            pltpu.VMEM((4, 4, 16, width), BF16),
            pltpu.VMEM((2, 4, 16, width), BF16),
        ]
    return pl.pallas_call(
        reduce_kernel,
        in_specs=[ANY, ANY, VMEM, ANY, ANY],
        out_specs=[VMEM, VMEM, VMEM],
        out_shape=[
            jax.ShapeDtypeStruct((8, 1024), F32),
            jax.ShapeDtypeStruct((8, 1024), F32),
            jax.ShapeDtypeStruct((8, BLK), F32),
        ],
        scratch_shapes=scratch
        + [
            pltpu.VMEM((2, 8, 1024), F32),
            pltpu.VMEM((8, 1024), F32),
            DMA((3,)), DMA((3,)),
            DMA((12,)), DMA((12,)), DMA((12,)), DMA((12,)), DMA((12,)), DMA((12,)),
            DMA((1,)), DMA((1,)), DMA((8,)), DMA((1,)), DMA((5,)),
        ],
        compiler_params=pltpu.CompilerParams(
            collective_id=1, has_side_effects=True, vmem_limit_bytes=60 * 1024 * 1024
        ),
        name="reduce",
    )(stiff, mass, diag, cm, rm)


def body(inv_interior, coupling, boundary_stiff, mass_interior, mass_boundary, block_map, modes):
    a2, b2, ma2, mb2, cm, rm = exchange(
        block_map, inv_interior, coupling, boundary_stiff, mass_interior, mass_boundary, modes.T
    )
    stiff_tile, mass_tile, diag = assemble(a2, b2, ma2, mb2)
    stiff, mass, diagonal = reduce_parts(stiff_tile, mass_tile, diag, cm, rm)
    return stiff_tile, mass_tile, stiff, mass, diagonal[0]


def solution(mesh):
    both = ("row", "col")
    return jax.shard_map(
        body,
        mesh=mesh,
        in_specs=(
            P(both, None, None),
            P(both, None, None),
            P(both, None, None),
            P(both, None),
            P(both, None),
            P(both, None),
            P("col", "row"),
        ),
        out_specs=(
            P("row", "col"),
            P("row", "col"),
            P(both, None),
            P(both, None),
            P(both),
        ),
        check_vma=False,
    )
```

time: 340 us -> 191 us (0.56)
  Pallas kernels: 332 us -> 186 us
    pallas_call x4 -> x3, Pallas kernels: 332 us -> 186 us  [the longest x1 129 us: exchange(): pl.pallas_call(exchange_kernel, in_specs=[pl.BlockSpec(memory_space=pltpu...]
where the time goes in v2:
time: 191 us; the launch traced here: 190 us
  Pallas kernels  186 us (97%)
  local copies, waits for them, and re-layouts  3.94 us (2%)
    pallas_call x1, Pallas kernels, exchange(): pl.pallas_call(exchange_kernel, in_specs=[pl.BlockSpec(memory_space=pltpu...  129 us
    pallas_call x1, Pallas kernels, reduce_parts(): pl.pallas_call(reduce_kernel, in_specs=[ANY, ANY, VMEM, ANY, ANY], out_sp...  47.8 us
    pallas_call x1, Pallas kernels, assemble(): pl.pallas_call(assemble_kernel, in_specs=[ANY] * 4, out_specs=[ANY, ANY,...  8.89 us

profile of v2, /device:TPU:1, one launch (start us, length us, event | category | flops | bytes accessed | tf_op | source)
XLA Modules:
  0.0 190.4 jit_solution(4439448669630216967)
XLA Ops:
  0.6 129.1 %exchange.1 = (bf16[8,16,128,128]{3,2,1,0:T(8,128)(2,1)}, bf16[16,8,128,128]{3,2,1,0:T(8,128)(2,1)}, s32[8,8,128]{2,1,0:T(8,128)}, s32[16,8,128]{2,1,0:T(8,128)}...) custom-call(s32[4,4]{1,0:T(4,128)} %map_ref.1, bf16[4,1024,1024]{2,1,0:T(8,128)(2,1)} %inv.1, ...), custom_call_target="tpu_custom_call" | custom-call | tf_op jit(solution)/shard_map/exchange/pallas_call | solution.py:369
  129.7 8.9 %assemble.1 = (bf16[1024,2048]{1,0:T(8,128)(2,1)}, bf16[1024,2048]{1,0:T(8,128)(2,1)}, f32[8,8,128]{2,1,0:T(8,128)}) custom-call(bf16[8,16,128,128]{3,2,1,0:T(8,128)(2,1)} %get-tuple-element.17.a2, bf16[16,8,128,128]{3,2,1,0:T(8,128)(2,1)} %get-tuple-element.18.b2, s32[8,8,128]{2,1,0:T(8,128)} %get-tuple-element.19.ma2, s32[16,8,128]{2,1,0:T(8,128)} %get-tuple-element.20.mb2), custom_call_target="tpu_custom_call" | custom-call | tf_op jit(solution)/shard_map/assemble/pallas_call | solution.py:491
  138.6 47.8 %reduce.1 = (f32[8,1024]{1,0:T(8,128)}, f32[8,1024]{1,0:T(8,128)}, f32[8,128]{1,0:T(8,128)}) custom-call(bf16[1024,2048]{1,0:T(8,128)(2,1)} %get-tuple-element.34.stiff, bf16[1024,2048]{1,0:T(8,128)(2,1)} %get-tuple-element.35.mass, f32[8,8,128]{2,1,0:T(8,128)} %get-tuple-element.23.diag, bf16[2,16,64,1024]{3,2,1,0:T(8,128)(2,1)} %get-tuple-element.24.cm, ...), custom_call_target="tpu_custom_call" | custom-call | tf_op jit(solution)/shard_map/reduce/pallas_call | solution.py:710
  186.5 1.2 slice_bitcast_fusion
  187.7 1.4 copy.14
  189.1 1.4 copy.15

commit v3 on v2

--- a/solution.py
+++ b/solution.py
@@ -9,6 +9,8 @@
 
 MESH = pl.DeviceIdType.MESH
 BLK = 128
+LIFT = 32
+REST = BLK - LIFT
 F32 = jnp.float32
 BF16 = jnp.bfloat16
 I32 = jnp.int32
@@ -96,7 +98,7 @@
         )
         stiffness = stiffness.astype(BF16)
         for a in range(4):
-            nat_a[s * 4 + a] = stiffness[a * BLK : (a + 1) * BLK, :]
+            nat_a[s * 4 + a, 0:BLK, :] = stiffness[a * BLK : (a + 1) * BLK, :]
         static_t = static.T
         weighted_t = (static_t.astype(F32) * mi_ref[pl.ds(s, 1), :]).astype(BF16)
         mass = lax.dot_general(
@@ -107,11 +109,15 @@
         col_ids = lax.broadcasted_iota(I32, (width, width), 1)
         mass = mass + jnp.where(row_ids == col_ids, mb_ref[pl.ds(s, 1), :], F32(0.0))
         mass = mass.astype(BF16)
-        for b in range(4):
-            nat_b[s * 4 + b] = mass[:, b * BLK : (b + 1) * BLK]
+        for a in range(4):
+            lifted = a * BLK + LIFT
+            nat_a[s * 4 + a, BLK : BLK + LIFT, :] = mass[a * BLK : lifted, :]
+            for b in range(4):
+                nat_b[s * 4 + b, a * REST : (a + 1) * REST, :] = mass[
+                    lifted : (a + 1) * BLK, b * BLK : (b + 1) * BLK
+                ]
         return carry
 
-    lax.fori_loop(0, 1, condense, 0)
     pl.semaphore_wait(barrier, 22)
     for d in (1, 3, 2):
         for h in range(2):
@@ -123,7 +129,7 @@
                     m1s.at[n], m1r.at[n], r, col,
                 )
             )
-    lax.fori_loop(1, 3, condense, 0)
+    lax.fori_loop(0, 2, condense, 0)
     for copy in own_modes:
         copy.wait()
     for d in (0, 1, 3, 2):
@@ -137,7 +143,7 @@
                 r = at.row_at(0, e) if h == 0 else at.row_at(e, 0)
                 n = h * 12 + d * 3 + e - 1
                 go(remote(cm.at[h, back], cm.at[h, back], m2s.at[n], m2r.at[n], r, col))
-    lax.fori_loop(3, 4, condense, 0)
+    lax.fori_loop(2, 4, condense, 0)
 
     lines = lax.broadcasted_iota(I32, (8, BLK), 0)
 
@@ -228,7 +234,7 @@
         base = lax.rem(meta[4:5, :], 8) * 16 + 1
         for o in range(8):
             c = at.col_at(*COL_OFFS[o])
-            total = jnp.zeros((BLK, BLK), BF16)
+            total = jnp.zeros((BLK + LIFT, BLK), BF16)
             slot = jnp.zeros((1, BLK), I32)
             for b in range(4):
                 q = meta[b : b + 1, :]
@@ -243,7 +249,7 @@
     def pack_b(n, carry):
         def each(o, inside):
             r = lax.rem(at.z + lax.div(o, 4), 4) * 4 + lax.rem(at.y + lax.rem(o, 4), 4)
-            total = jnp.zeros((BLK, BLK), BF16)
+            total = jnp.zeros((REST, BLK), BF16)
             slot = jnp.zeros((1, BLK), I32)
             for h in range(2):
                 meta = arr_mb[n, h]
@@ -252,7 +258,7 @@
                     p = meta[a : a + 1, :]
                     hit = lax.div(p, 8) == r
                     mask = jnp.where(hit, F32(1.0), F32(0.0)).astype(BF16)
-                    total = total + arr_b[n, h, a * BLK : (a + 1) * BLK, :] * mask
+                    total = total + arr_b[n, h, a * REST : (a + 1) * REST, :] * mask
                     slot = jnp.where(hit, base + lax.rem(p, 8) * 16, slot)
             pk_b[o, n] = total
             pk_mb[o] = pk_mb[o] + jnp.where(lanes == n, slot, 0)
@@ -371,8 +377,8 @@
         in_specs=[pl.BlockSpec(memory_space=pltpu.SMEM), ANY, ANY, ANY, VMEM, VMEM, ANY],
         out_specs=[ANY] * 6,
         out_shape=[
-            jax.ShapeDtypeStruct((8, 16, BLK, BLK), BF16),
-            jax.ShapeDtypeStruct((16, 8, BLK, BLK), BF16),
+            jax.ShapeDtypeStruct((8, 16, BLK + LIFT, BLK), BF16),
+            jax.ShapeDtypeStruct((16, 8, REST, BLK), BF16),
             jax.ShapeDtypeStruct((8, 8, BLK), I32),
             jax.ShapeDtypeStruct((16, 8, BLK), I32),
             jax.ShapeDtypeStruct((2, 16, 64, 1024), BF16),
@@ -382,18 +388,18 @@
             pltpu.VMEM((subs, inside, inside), BF16),
             pltpu.VMEM((subs, inside, edge), BF16),
             pltpu.VMEM((subs, edge, edge), BF16),
-            pltpu.VMEM((16, BLK, edge), BF16),
-            pltpu.VMEM((16, edge, BLK), BF16),
-            pltpu.VMEM((16, BLK, edge), BF16),
-            pltpu.VMEM((8, 2, edge, BLK), BF16),
+            pltpu.VMEM((16, BLK + LIFT, edge), BF16),
+            pltpu.VMEM((16, 4 * REST, BLK), BF16),
+            pltpu.VMEM((16, BLK + LIFT, edge), BF16),
+            pltpu.VMEM((8, 2, 4 * REST, BLK), BF16),
             pltpu.VMEM((16, 8, BLK), I32),
             pltpu.VMEM((8, 2, 8, BLK), I32),
-            pltpu.VMEM((16, BLK, edge), BF16),
-            pltpu.VMEM((8, 2, edge, BLK), BF16),
+            pltpu.VMEM((16, BLK + LIFT, edge), BF16),
+            pltpu.VMEM((8, 2, 4 * REST, BLK), BF16),
             pltpu.VMEM((16, 8, BLK), I32),
             pltpu.VMEM((8, 2, 8, BLK), I32),
-            pltpu.VMEM((8, 16, BLK, BLK), BF16),
-            pltpu.VMEM((16, 8, BLK, BLK), BF16),
+            pltpu.VMEM((8, 16, BLK + LIFT, BLK), BF16),
+            pltpu.VMEM((16, 8, REST, BLK), BF16),
             pltpu.VMEM((8, 8, BLK), I32),
             pltpu.VMEM((16, 8, BLK), I32),
             DMA((3, 4)),
@@ -433,15 +439,21 @@
         acc[n] = jnp.zeros((BLK, BLK), F32)
         return carry
 
-    def gather(base, blocks, slots, senders, each):
-        def one(n, carry):
-            for u in range(4):
-                o, k = lax.div(n * 4, each), lax.rem(n * 4, each) + u
-                slot = slots[o, 0, k] + base
-                acc[slot] = acc[slot] + blocks[o, k].astype(F32)
-            return carry
-
-        lax.fori_loop(0, senders * each // 4, one, 0)
+    def gather_a(n, carry):
+        for u in range(4):
+            o, k = lax.div(n, 4), lax.rem(n, 4) * 4 + u
+            slot = sa[o, 0, k]
+            acc[slot] = acc[slot] + va[o, k, 0:BLK, :].astype(F32)
+            lifted = acc[slot + 129, 0:LIFT, :] + va[o, k, BLK : BLK + LIFT, :].astype(F32)
+            acc[slot + 129, 0:LIFT, :] = lifted
+        return carry
+
+    def gather_b(n, carry):
+        for u in range(4):
+            o, k = lax.div(n, 2), lax.rem(n, 2) * 4 + u
+            slot = sb[o, 0, k] + 129
+            acc[slot, LIFT:BLK, :] = acc[slot, LIFT:BLK, :] + vb[o, k].astype(F32)
+        return carry
 
     def round_to(base, out):
         def one(p, carry):
@@ -455,13 +467,13 @@
     lax.fori_loop(0, 258, clear, 0)
     copies[0].wait()
     copies[1].wait()
-    gather(0, va, sa, 8, 16)
+    lax.fori_loop(0, 32, gather_a, 0)
     round_to(0, tile)
     out_stiff = pltpu.make_async_copy(tile, stiff_out, sems.at[4])
     out_stiff.start()
     copies[2].wait()
     copies[3].wait()
-    gather(129, vb, sb, 16, 8)
+    lax.fori_loop(0, 32, gather_b, 0)
     round_to(129, mass_tile)
     row_ids = lax.broadcasted_iota(I32, (BLK, BLK), 0)
     col_ids = lax.broadcasted_iota(I32, (BLK, BLK), 1)
@@ -498,8 +510,8 @@
             jax.ShapeDtypeStruct((8, 8, BLK), F32),
         ],
         scratch_shapes=[
-            pltpu.VMEM((8, 16, BLK, BLK), BF16),
-            pltpu.VMEM((16, 8, BLK, BLK), BF16),
+            pltpu.VMEM((8, 16, BLK + LIFT, BLK), BF16),
+            pltpu.VMEM((16, 8, REST, BLK), BF16),
             pltpu.SMEM((8, 8, BLK), I32),
             pltpu.SMEM((16, 8, BLK), I32),
             pltpu.VMEM((258, BLK, BLK), F32),
@@ -512,7 +524,8 @@
     )(a2, b2, ma2, mb2)
 
 
-GROUPS = ((0, 6, "zyx"), (6, 6, "yxz"), (12, 4, "xzy"))
+GROUPS = ("zyx", "yxz", "xzy", "zyx")
+WIDTH = 256
 
 
 def reduce_kernel(
@@ -520,9 +533,9 @@
     stiff_out, mass_out, diag_out,
     tiles, vcm, vrm, *rest,
 ):
-    bufs = [rest[7 * j : 7 * j + 7] for j in range(3)]
-    send_last, arr_last = rest[21:23]
-    ns, nr, s1, r1, s2, r2, s3, r3, ls, lr, ds, dr, local = rest[23:]
+    bufs = [rest[7 * j : 7 * j + 7] for j in range(4)]
+    send_last, arr_last = rest[28:30]
+    ns, nr, s1, r1, s2, r2, s3, r3, ls, lr, ds, dr, local = rest[30:]
     at = Place()
     row, col = at.row, at.col
     half = lax.rem(row, 2)
@@ -548,25 +561,28 @@
     for dx, dk in COL_OFFS[1:]:
         pl.semaphore_signal(barrier, inc=1, device_id=(row, at.col_at(dx, dk)), device_id_type=MESH)
     sibling = at.col_at(0, 1)
+    depth = cm.shape[2]
     loads = [
-        pltpu.make_async_copy(cm, vcm, local.at[0]),
-        pltpu.make_async_copy(stiff, tiles.at[0], local.at[1]),
-        pltpu.make_async_copy(mass, tiles.at[1], local.at[2]),
+        pltpu.make_async_copy(cm.at[h], vcm.at[:, pl.ds(h * depth, depth)], local.at[h])
+        for h in range(2)
+    ] + [
+        pltpu.make_async_copy(stiff, tiles.at[0], local.at[2]),
+        pltpu.make_async_copy(mass, tiles.at[1], local.at[3]),
     ]
     for copy in loads:
         copy.start()
 
     @pl.when(holder)
     def _():
-        pltpu.make_async_copy(cm.at[half], vrm, local.at[3]).start()
+        pltpu.make_async_copy(cm.at[half], vrm, local.at[4]).start()
 
     @pl.when(jnp.logical_not(holder))
     def _():
-        pltpu.make_async_copy(rm, vrm, local.at[3]).start()
+        pltpu.make_async_copy(rm, vrm, local.at[4]).start()
 
     for copy in loads:
         copy.wait()
-    pltpu.make_async_copy(rm, vrm, local.at[3]).wait()
+    pltpu.make_async_copy(rm, vrm, local.at[4]).wait()
 
     @pl.when(holder)
     def _():
@@ -591,36 +607,32 @@
     def _():
         for o in range(1, 8):
             diag_copy(o).start()
-        own = pltpu.make_async_copy(diag.at[col], diag_out, local.at[4])
+        own = pltpu.make_async_copy(diag.at[col], diag_out, local.at[5])
         own.start()
         own.wait()
 
-    def product(which, j):
-        first, count, _ = GROUPS[j]
-        depth = vcm.shape[3]
-        total = None
-        for h in range(2):
-            modes = vcm[h, first : first + count].reshape(count * 64, depth)
-            add = lax.dot_general(
-                tiles[which, :, h * depth : (h + 1) * depth], modes,
-                (((1,), (1,)), ((), ())), preferred_element_type=F32,
-            )
-            total = add if total is None else total + add
-        left = vrm[...].reshape(1024, depth)
-        return jnp.dot(left, total.astype(BF16), preferred_element_type=F32)
+    def product(which, pair):
+        modes = vcm[pair * 2 * WIDTH : (pair + 1) * 2 * WIDTH, :]
+        image = lax.dot_general(
+            tiles[which], modes, (((1,), (1,)), ((), ())), preferred_element_type=F32
+        )
+        return jnp.dot(vrm[...], image.astype(BF16), preferred_element_type=F32)
 
     near = []
-    for j in range(3):
-        out_near, in_near = bufs[j][0], bufs[j][1]
-        out_near[...] = product(1 - at.k, j).astype(BF16)
-        copy = remote(out_near, in_near, ns.at[j], nr.at[j], row, sibling)
-        copy.start()
-        near.append(copy)
+    for pair in range(2):
+        theirs = product(1 - at.k, pair).astype(BF16)
+        for side in range(2):
+            j = pair * 2 + side
+            out_near, in_near = bufs[j][:2]
+            out_near[...] = theirs[:, side * WIDTH : (side + 1) * WIDTH]
+            copy = remote(out_near, in_near, ns.at[j], nr.at[j], row, sibling)
+            copy.start()
+            near.append(copy)
     sends = []
 
     def leg(j, level, src, dst, ssem, rsem):
-        axis = GROUPS[j][2][level]
-        dims = sorted(GROUPS[j][2][level:], key="zyx".index)
+        axis = GROUPS[j][level]
+        dims = sorted(GROUPS[j][level:], key="zyx".index)
         spot = dims.index(axis)
         arriving = []
         for d in range(1, 4):
@@ -641,31 +653,32 @@
         return total
 
     first_legs = []
-    for j in range(3):
-        _, in_near, near_sum, arr1, _, _, _ = bufs[j]
-        width = GROUPS[j][1] * 64
-        here = product(at.k, j)
-        near[j].wait_recv()
-        total = (here + in_near[...].astype(F32)).astype(BF16)
-        near_sum[...] = total.reshape(4, 4, 4, 16, width)
-        first_legs.append(leg(j, 0, near_sum, arr1, s1, r1))
+    for pair in range(2):
+        ours = product(at.k, pair)
+        for side in range(2):
+            j = pair * 2 + side
+            _, in_near, near_sum, arr1, _, _, _ = bufs[j]
+            near[j].wait_recv()
+            total = ours[:, side * WIDTH : (side + 1) * WIDTH] + in_near[...].astype(F32)
+            near_sum[...] = total.astype(BF16).reshape(4, 4, 4, 16, WIDTH)
+            first_legs.append(leg(j, 0, near_sum, arr1, s1, r1))
     second_legs = []
-    for j in range(3):
+    for j in range(4):
         _, _, near_sum, arr1, sum1, arr2, _ = bufs[j]
         arriving, own = first_legs[j]
         sum1[...] = summed(near_sum, own, arr1, arriving).astype(BF16)
         second_legs.append(leg(j, 1, sum1, arr2, s2, r2))
     third_legs = []
-    for j in range(3):
+    for j in range(4):
         sum1, arr2, last = bufs[j][4:]
         arriving, own = second_legs[j]
         last[0] = summed(sum1, own, arr2, arriving).astype(BF16)
         third_legs.append(leg(j, 2, last.at[0], last.at[1], s3, r3))
-    for j in range(3):
+    for j in range(4):
         last = bufs[j][6]
         arriving, own = third_legs[j]
         total = summed(last.at[0], own, last.at[1], arriving)
-        cols = slice(GROUPS[j][0] * 64, (GROUPS[j][0] + GROUPS[j][1]) * 64)
+        cols = slice(j * WIDTH, (j + 1) * WIDTH)
         send_last[0, :, cols] = total[0:8, :]
         send_last[1, :, cols] = total[8:16, :]
     final = remote(send_last.at[1 - at.k], arr_last, ls.at[0], lr.at[0], row, sibling)
@@ -693,19 +706,18 @@
 def reduce_parts(stiff, mass, diag, cm, rm):
     scratch = [
         pltpu.VMEM((2, 1024, 2048), BF16),
-        pltpu.VMEM((2, 16, 64, 1024), BF16),
-        pltpu.VMEM((16, 64, 1024), BF16),
+        pltpu.VMEM((1024, 2048), BF16),
+        pltpu.VMEM((1024, 1024), BF16),
     ]
-    for _, count, _ in GROUPS:
-        width = count * 64
+    for _ in GROUPS:
         scratch += [
-            pltpu.VMEM((1024, width), BF16),
-            pltpu.VMEM((1024, width), BF16),
-            pltpu.VMEM((4, 4, 4, 16, width), BF16),
-            pltpu.VMEM((4, 4, 4, 16, width), BF16),
-            pltpu.VMEM((4, 4, 16, width), BF16),
-            pltpu.VMEM((4, 4, 16, width), BF16),
-            pltpu.VMEM((2, 4, 16, width), BF16),
+            pltpu.VMEM((1024, WIDTH), BF16),
+            pltpu.VMEM((1024, WIDTH), BF16),
+            pltpu.VMEM((4, 4, 4, 16, WIDTH), BF16),
+            pltpu.VMEM((4, 4, 4, 16, WIDTH), BF16),
+            pltpu.VMEM((4, 4, 16, WIDTH), BF16),
+            pltpu.VMEM((4, 4, 16, WIDTH), BF16),
+            pltpu.VMEM((2, 4, 16, WIDTH), BF16),
         ]
     return pl.pallas_call(
         reduce_kernel,
@@ -720,9 +732,9 @@
         + [
             pltpu.VMEM((2, 8, 1024), F32),
             pltpu.VMEM((8, 1024), F32),
-            DMA((3,)), DMA((3,)),
-            DMA((12,)), DMA((12,)), DMA((12,)), DMA((12,)), DMA((12,)), DMA((12,)),
-            DMA((1,)), DMA((1,)), DMA((8,)), DMA((1,)), DMA((5,)),
+            DMA((4,)), DMA((4,)),
+            DMA((16,)), DMA((16,)), DMA((16,)), DMA((16,)), DMA((16,)), DMA((16,)),
+            DMA((1,)), DMA((1,)), DMA((8,)), DMA((1,)), DMA((6,)),
         ],
         compiler_params=pltpu.CompilerParams(
             collective_id=1, has_side_effects=True, vmem_limit_bytes=60 * 1024 * 1024
@@ -736,7 +748,9 @@
         block_map, inv_interior, coupling, boundary_stiff, mass_interior, mass_boundary, modes.T
     )
     stiff_tile, mass_tile, diag = assemble(a2, b2, ma2, mb2)
-    stiff, mass, diagonal = reduce_parts(stiff_tile, mass_tile, diag, cm, rm)
+    stiff, mass, diagonal = reduce_parts(
+        stiff_tile, mass_tile, diag, cm.reshape(2, 1024, 1024), rm.reshape(1024, 1024)
+    )
     return stiff_tile, mass_tile, stiff, mass, diagonal[0]
 
 

time: 191 us -> 183 us (0.958)
  Pallas kernels: 186 us -> 178 us
    pallas_call x1, Pallas kernels: 129 us -> 118 us  [exchange(): pl.pallas_call(exchange_kernel, in_specs=[pl.BlockSpec(memory_space=pltpu...]
    pallas_call x1, Pallas kernels: 47.8 us -> 50.3 us  [reduce_parts(): pl.pallas_call(reduce_kernel, in_specs=[ANY, ANY, VMEM, ANY, ANY], out_sp...]
where the time goes in v3:
time: 183 us; the launch traced here: 182 us
  Pallas kernels  178 us (97%)
  local copies, waits for them, and re-layouts  3.94 us (2%)
    pallas_call x1, Pallas kernels, exchange(): pl.pallas_call(exchange_kernel, in_specs=[pl.BlockSpec(memory_space=pltpu...  118 us
    pallas_call x1, Pallas kernels, reduce_parts(): pl.pallas_call(reduce_kernel, in_specs=[ANY, ANY, VMEM, ANY, ANY], out_sp...  50.3 us
    pallas_call x1, Pallas kernels, assemble(): pl.pallas_call(assemble_kernel, in_specs=[ANY] * 4, out_specs=[ANY, ANY,...  9.2 us

profile of v3, /device:TPU:1, one launch (start us, length us, event | category | flops | bytes accessed | tf_op | source)
XLA Modules:
  0.0 182.3 jit_solution(12476316584047558583)
XLA Ops:
  0.6 118.3 %exchange.1 = (bf16[8,16,160,128]{3,2,1,0:T(8,128)(2,1)}, bf16[16,8,96,128]{3,2,1,0:T(8,128)(2,1)}, s32[8,8,128]{2,1,0:T(8,128)}, s32[16,8,128]{2,1,0:T(8,128)},...) custom-call(s32[4,4]{1,0:T(4,128)} %map_ref.1, bf16[4,1024,1024]{2,1,0:T(8,128)(2,1)} %inv.1, ...), custom_call_target="tpu_custom_call" | custom-call | tf_op jit(solution)/shard_map/exchange/pallas_call | solution.py:375
  118.9 9.2 %assemble.1 = (bf16[1024,2048]{1,0:T(8,128)(2,1)}, bf16[1024,2048]{1,0:T(8,128)(2,1)}, f32[8,8,128]{2,1,0:T(8,128)}) custom-call(bf16[8,16,160,128]{3,2,1,0:T(8,128)(2,1)} %get-tuple-element.17.a2, bf16[16,8,96,128]{3,2,1,0:T(8,128)(2,1)} %get-tuple-element.18.b2, s32[8,8,128]{2,1,0:T(8,128)} %get-tuple-element.19.ma2, s32[16,8,128]{2,1,0:T(8,128)} %get-tuple-element.20.mb2), custom_call_target="tpu_custom_call" | custom-call | tf_op jit(solution)/shard_map/assemble/pallas_call | solution.py:503
  128.1 50.3 %reduce.1 = (f32[8,1024]{1,0:T(8,128)}, f32[8,1024]{1,0:T(8,128)}, f32[8,128]{1,0:T(8,128)}) custom-call(bf16[1024,2048]{1,0:T(8,128)(2,1)} %get-tuple-element.34.stiff, bf16[1024,2048]{1,0:T(8,128)(2,1)} %get-tuple-element.35.mass, f32[8,8,128]{2,1,0:T(8,128)} %get-tuple-element.23.diag, bf16[2,1024,1024]{2,1,0:T(8,128)(2,1)} %bitcast.5, ...), custom_call_target="tpu_custom_call" | custom-call | tf_op jit(solution)/shard_map/reduce/pallas_call | solution.py:722
  178.4 1.2 slice_bitcast_fusion
  179.6 1.4 copy.14
  180.9 1.4 copy.15

commit v4 on v3

--- a/solution.py
+++ b/solution.py
@@ -9,7 +9,7 @@
 
 MESH = pl.DeviceIdType.MESH
 BLK = 128
-LIFT = 32
+LIFT = 16
 REST = BLK - LIFT
 F32 = jnp.float32
 BF16 = jnp.bfloat16

time: 183 us -> 181 us (0.989)
  Pallas kernels: 178 us -> 176 us
    pallas_call x1, Pallas kernels: 50.3 us -> 45.5 us  [reduce_parts(): pl.pallas_call(reduce_kernel, in_specs=[ANY, ANY, VMEM, ANY, ANY], out_sp...]
    pallas_call x1, Pallas kernels: 118 us -> 121 us  [exchange(): pl.pallas_call(exchange_kernel, in_specs=[pl.BlockSpec(memory_space=pltpu...]
where the time goes in v4:
time: 181 us
  Pallas kernels  176 us (97%)
  local copies, waits for them, and re-layouts  3.93 us (2%)
    pallas_call x1, Pallas kernels, exchange(): pl.pallas_call(exchange_kernel, in_specs=[pl.BlockSpec(memory_space=pltpu...  121 us
    pallas_call x1, Pallas kernels, reduce_parts(): pl.pallas_call(reduce_kernel, in_specs=[ANY, ANY, VMEM, ANY, ANY], out_sp...  45.5 us
    pallas_call x1, Pallas kernels, assemble(): pl.pallas_call(assemble_kernel, in_specs=[ANY] * 4, out_specs=[ANY, ANY,...  9.07 us

profile of v4, /device:TPU:1, one launch (start us, length us, event | category | flops | bytes accessed | tf_op | source)
XLA Modules:
  0.0 180.6 jit_solution(5840793236994838770)
XLA Ops:
  0.6 121.5 %exchange.1 = (bf16[8,16,144,128]{3,2,1,0:T(8,128)(2,1)}, bf16[16,8,112,128]{3,2,1,0:T(8,128)(2,1)}, s32[8,8,128]{2,1,0:T(8,128)}, s32[16,8,128]{2,1,0:T(8,128)}...) custom-call(s32[4,4]{1,0:T(4,128)} %map_ref.1, bf16[4,1024,1024]{2,1,0:T(8,128)(2,1)} %inv.1, ...), custom_call_target="tpu_custom_call" | custom-call | tf_op jit(solution)/shard_map/exchange/pallas_call | solution.py:375
  122.1 9.1 %assemble.1 = (bf16[1024,2048]{1,0:T(8,128)(2,1)}, bf16[1024,2048]{1,0:T(8,128)(2,1)}, f32[8,8,128]{2,1,0:T(8,128)}) custom-call(bf16[8,16,144,128]{3,2,1,0:T(8,128)(2,1)} %get-tuple-element.17.a2, bf16[16,8,112,128]{3,2,1,0:T(8,128)(2,1)} %get-tuple-element.18.b2, s32[8,8,128]{2,1,0:T(8,128)} %get-tuple-element.19.ma2, s32[16,8,128]{2,1,0:T(8,128)} %get-tuple-element.20.mb2), custom_call_target="tpu_custom_call" | custom-call | tf_op jit(solution)/shard_map/assemble/pallas_call | solution.py:503
  131.2 45.5 %reduce.1 = (f32[8,1024]{1,0:T(8,128)}, f32[8,1024]{1,0:T(8,128)}, f32[8,128]{1,0:T(8,128)}) custom-call(bf16[1024,2048]{1,0:T(8,128)(2,1)} %get-tuple-element.34.stiff, bf16[1024,2048]{1,0:T(8,128)(2,1)} %get-tuple-element.35.mass, f32[8,8,128]{2,1,0:T(8,128)} %get-tuple-element.23.diag, bf16[2,1024,1024]{2,1,0:T(8,128)(2,1)} %bitcast.5, ...), custom_call_target="tpu_custom_call" | custom-call | tf_op jit(solution)/shard_map/reduce/pallas_call | solution.py:722
  176.7 1.2 slice_bitcast_fusion
  177.9 1.4 copy.14
  179.3 1.4 copy.15
